TPU v7x, 128 devices: a whole 4x4x4 slice. The times are simulated.
128 devices in a mesh: blk: 32 (over x, z, core), grp: 4 (over y).
Axes of the slice: x: 4, y: 4, z: 4, core: 2. Of those that a mesh axis runs over, the one named last changes fastest.
Arguments:
- statistics: float32 [4, 64, 512, 512], P('grp', 'blk'), as said below
- gradients: bfloat16 [4, 16, 512, 14336], P('grp', None, None, 'blk'), may hold values from -6 to 6
- live_counts: int32 [4, 32], P('grp'), may hold values from 0 to 2, as said below
- slot_row: int32 [4, 64], P('grp'), may hold values from 0 to 15, as said below
- sweeps: int32 [4, 64], P('grp', 'blk'), may hold values from 1 to 2, as said below
Outputs:
- updates: bfloat16 [4, 16, 512, 14336], P('grp', None, None, 'blk')
- off_max: float32 [2], replicated
Inputs may be any that keep to these rules, and one draw needn't show every extreme that they name: `live_counts`: the live slots of one index of grp number exactly 16; in every draw some device of each grp index has 2 live slots. `slot_row`: over the live slots of one index of grp each row block 0 to 15 appears exactly once. In each index of grp some live slot has 2 sweeps. `statistics`: every block is symmetric positive definite.
All inputs are finite; a program needn't handle non-finite values.
Results may differ from a plain program's by a relative error of at most 0.0051.
Values may be sent and summed in bfloat16 or wider, within the bound.
A program may use at most 192 MiB of HBM per device.

v0:
```python
import functools

import jax
import jax.numpy as jnp
from jax import lax
from jax.experimental import pallas as pl
from jax.experimental.pallas import tpu as pltpu
from jax.sharding import PartitionSpec as P

MAXS = 2

damping = 0.01
pairings = ((0, 1, 2, 3), (0, 2, 1, 3), (0, 3, 1, 2))
kappa_steps = (1.16, 1.74, 3.17, 6.2, 12.3, 24.5, 49.0, 98.0, 196.0)
bf16 = jnp.bfloat16
f32 = jnp.float32


def split(values):
    high = values.astype(bf16)
    return high, (values - high.astype(f32)).astype(bf16)


def left_parts(parts):
    high, low = parts
    return jnp.concatenate([high, high, low], axis=1)


def right_parts(parts):
    high, low = parts
    return jnp.concatenate([high, low, high], axis=0)


def dot(left, right):
    return jnp.dot(left, right, preferred_element_type=f32)


def dot3(left, right):
    return dot(left_parts(split(left)), right_parts(split(right)))


def eye_mask(size):
    shape = (size, size)
    return lax.broadcasted_iota(jnp.int32, shape, 0) == lax.broadcasted_iota(jnp.int32, shape, 1)


def angles_of(lower, coupling, upper, on_diagonal):
    lower_diag = jnp.sum(jnp.where(on_diagonal, lower, 0.0), axis=1, keepdims=True)
    upper_diag = jnp.sum(jnp.where(on_diagonal, upper, 0.0), axis=0, keepdims=True)
    difference = upper_diag - lower_diag
    total = lower_diag + upper_diag
    bottom = difference * difference + 4.0 * coupling * coupling + damping * (total * total)
    return coupling * difference / bottom


def jacobi_kernel(
    stats_ref, counts_ref, sweeps_ref, packed_ref, off_ref,
    mat, vec_high, vec_low, mid_high, mid_low, angle, powers,
):
    slot_count, size, _ = mat.shape
    width = size // 4
    rank = lax.axis_index("blk")
    own_live = counts_ref[0, rank]
    on_diagonal = eye_mask(width)
    identity = jnp.where(on_diagonal, 1.0, 0.0).astype(f32)

    def span(member):
        return pl.ds(member * width, width)

    def one_round(slots, pairing):
        pairs = (pairing[:2], pairing[2:])
        chains = [(at, slot, half) for at, slot in enumerate(slots) for half in range(2)]
        outers = []
        peak = jnp.zeros((1, width), f32)
        for at, slot, half in chains:
            first, second = pairs[half]
            angles = angles_of(
                mat[slot, span(first), span(first)],
                mat[slot, span(first), span(second)],
                mat[slot, span(second), span(second)],
                on_diagonal,
            )
            angle[2 * at + half] = angles
            outer = dot3(angles, angles.T)
            outers.append(outer)
            peak = jnp.maximum(peak, jnp.sum(jnp.abs(outer), axis=0, keepdims=True))
        kappa = 1.0 + 0.26 * jnp.max(peak)
        count = jnp.int32(0)
        for bound in kappa_steps:
            count = count + (kappa > bound).astype(jnp.int32)
        scale = 2.0 / (1.0 + jnp.full((1, width), kappa))
        for at, slot, half in chains:
            error = (1.0 - scale) * identity - (0.25 * scale) * outers[2 * at + half]
            powers[2 * at + half, :, :width] = scale * (identity + error)
            powers[2 * at + half, :, width:] = dot3(error, error)

        def double(step, carry):
            for at, slot, half in chains:
                both = powers[2 * at + half]
                high, low = split(both)
                product = dot(
                    left_parts((high[:, width:], low[:, width:])), right_parts((high, low))
                )
                powers[2 * at + half, :, :width] = both[:, :width] + product[:, :width]
                powers[2 * at + half, :, width:] = product[:, width:]
            return carry

        lax.fori_loop(0, count, double, 0)

        flips = {}
        for at, slot, half in chains:
            first, second = pairs[half]
            angles = angle[2 * at + half]
            inverse = powers[2 * at + half, :, :width]
            inverse = inverse + dot(
                inverse.astype(bf16), powers[2 * at + half, :, width:].astype(bf16)
            )
            top_right = dot3(inverse, angles)
            flip_right = top_right.T
            low_right = identity - 0.5 * dot3(angles.T, top_right)
            top = split(2.0 * inverse - identity)
            right = split(top_right)
            flip = split(flip_right)
            low = split(low_right)

            def square(kind, flipped):
                above, below = (-right[kind], flip[kind]) if flipped else (right[kind], -flip[kind])
                return jnp.concatenate(
                    [
                        jnp.concatenate([top[kind], above], axis=1),
                        jnp.concatenate([below, low[kind]], axis=1),
                    ],
                    axis=0,
                )

            flips[at, half] = left_parts((square(0, True), square(1, True)))
            rotation = right_parts((square(0, False), square(1, False)))
            for members in (pairs[0],) if half == 0 else pairs:
                rows = jnp.concatenate(
                    [
                        jnp.concatenate(
                            [mat[slot, span(member), span(column)] for column in pairs[half]],
                            axis=1,
                        )
                        for member in members
                    ],
                    axis=0,
                )
                middle = split(dot(left_parts(split(rows)), rotation))
                for down, member in enumerate(members):
                    for across, column in enumerate(pairs[half]):
                        tall = slice(down * width, (down + 1) * width)
                        wide = slice(across * width, (across + 1) * width)
                        mid_high[slot, span(member), span(column)] = middle[0][tall, wide]
                        mid_low[slot, span(member), span(column)] = middle[1][tall, wide]
            columns = tuple(
                jnp.concatenate([ref[slot, :, span(first)], ref[slot, :, span(second)]], axis=1)
                for ref in (vec_high, vec_low)
            )
            turned = split(dot(left_parts(columns), rotation))
            for place, member in enumerate((first, second)):
                inner = slice(place * width, (place + 1) * width)
                vec_high[slot, :, span(member)] = turned[0][:, inner]
                vec_low[slot, :, span(member)] = turned[1][:, inner]
        for at, slot, half in chains:
            order = pairs[0] + pairs[1] if half == 0 else pairs[1]
            rows = tuple(
                jnp.concatenate(
                    [
                        jnp.concatenate(
                            [ref[slot, span(member), span(column)] for column in order], axis=1
                        )
                        for member in pairs[half]
                    ],
                    axis=0,
                )
                for ref in (mid_high, mid_low)
            )
            fresh = dot(flips[at, half], right_parts(rows))
            for down, member in enumerate(pairs[half]):
                for across, column in enumerate(order):
                    block = fresh[
                        down * width : (down + 1) * width, across * width : (across + 1) * width
                    ]
                    mat[slot, span(member), span(column)] = block
                    if across > 1:
                        mat[slot, span(column), span(member)] = block.T

    def measure(sweep, slot):
        outside = jnp.zeros((1, width), f32)
        inside = jnp.zeros((1, width), f32)
        for row in range(4):
            for column in range(4):
                squares = mat[slot, span(row), span(column)]
                squares = squares * squares
                if row == column:
                    own = jnp.where(on_diagonal, squares, 0.0)
                    inside += jnp.sum(own, axis=0, keepdims=True)
                    squares = jnp.where(on_diagonal, 0.0, squares)
                outside += jnp.sum(squares, axis=0, keepdims=True)
        off_total = jnp.sum(outside, axis=1, keepdims=True)
        total = off_total + jnp.sum(inside, axis=1, keepdims=True)
        norm = jnp.broadcast_to(jnp.sqrt(off_total / total), (1, width))
        row = pl.ds(sweep, 1)
        off_ref[row, :] = jnp.maximum(off_ref[row, :], norm)

    off_ref[...] = jnp.zeros_like(off_ref)
    packed_ref[...] = jnp.zeros_like(packed_ref)
    ident_rows = jnp.where(eye_mask(size), 1.0, 0.0).astype(bf16)

    for slot in range(slot_count):

        @pl.when(slot < own_live)
        def _():
            mat[slot] = stats_ref[0, slot]
            vec_high[slot] = ident_rows
            vec_low[slot] = jnp.zeros((size, size), bf16)

    def one_sweep(sweep, carry):
        active = [
            jnp.logical_and(slot < own_live, sweeps_ref[0, slot] > sweep)
            for slot in range(slot_count)
        ]

        def run(slots):
            for pairing in pairings:
                one_round(slots, pairing)
            for slot in slots:
                measure(sweep, slot)

        for slot in range(0, slot_count, 2):
            if slot + 1 == slot_count:
                pl.when(active[slot])(functools.partial(run, (slot,)))
                continue
            pl.when(jnp.logical_and(active[slot], active[slot + 1]))(
                functools.partial(run, (slot, slot + 1))
            )
            single = jnp.where(active[slot], slot, slot + 1)
            pl.when(jnp.logical_xor(active[slot], active[slot + 1]))(
                functools.partial(run, (single,))
            )
        return carry

    lax.fori_loop(0, MAXS, one_sweep, 0)

    for slot in range(slot_count):

        @pl.when(slot < own_live)
        def _():
            diagonal = jnp.concatenate(
                [
                    jnp.sum(
                        jnp.where(on_diagonal, mat[slot, span(member), span(member)], 0.0),
                        axis=0,
                        keepdims=True,
                    )
                    for member in range(4)
                ],
                axis=1,
            )
            scales = lax.rsqrt(jnp.sqrt(jnp.sqrt(diagonal)))
            vectors = vec_high[slot].astype(f32) + vec_low[slot].astype(f32)
            high, low = split(vectors * scales)
            left = jnp.concatenate([high, high, low], axis=1)
            right = jnp.concatenate([high, low, high], axis=1)
            start = 0
            for row in range(4):
                strip = lax.dot_general(
                    left[row * width : (row + 1) * width],
                    right[row * width :],
                    (((1,), (1,)), ((), ())),
                    preferred_element_type=f32,
                ).astype(bf16)
                for column in range(4 - row):
                    packed_ref[slot, start : start + width] = strip[
                        :, column * width : (column + 1) * width
                    ]
                    start += width


def jacobi(statistics, live_counts, sweeps, packed_rows):
    slot_count, size = statistics.shape[1], statistics.shape[2]
    width = size // 4
    vmem = pl.BlockSpec(memory_space=pltpu.VMEM)
    smem = pl.BlockSpec(memory_space=pltpu.SMEM)
    return pl.pallas_call(
        jacobi_kernel,
        name="jacobi",
        out_shape=(
            jax.ShapeDtypeStruct((slot_count, packed_rows, width), bf16),
            jax.ShapeDtypeStruct((8, width), f32),
        ),
        in_specs=[vmem, smem, smem],
        out_specs=(vmem, vmem),
        scratch_shapes=[
            pltpu.VMEM((slot_count, size, size), f32),
            pltpu.VMEM((slot_count, size, size), bf16),
            pltpu.VMEM((slot_count, size, size), bf16),
            pltpu.VMEM((slot_count, size, size), bf16),
            pltpu.VMEM((slot_count, size, size), bf16),
            pltpu.VMEM((4, width, width), f32),
            pltpu.VMEM((4, width, 2 * width), f32),
        ],
        compiler_params=pltpu.CompilerParams(vmem_limit_bytes=24 * 1024 * 1024),
        cost_estimate=pl.CostEstimate(
            flops=10**10, bytes_accessed=4 * slot_count * size * size, transcendentals=0
        ),
    )(statistics, live_counts, sweeps)


def far_first(count):
    return sorted(range(1, count), key=lambda step: abs(2 * step - count))


def exchange_kernel(
    peers, groups, packed_ref, peaks_ref, counts_ref, rows_ref, chosen_ref, off_ref,
    arrived, mine, gathered, peak_in, peak_own, peak_out,
    send_one, recv_one, send_two, recv_two, send_three, recv_three, send_peak, recv_peak, send_top, recv_top,
):
    rank = lax.axis_index("blk")
    group = lax.axis_index("grp")
    slot_count = packed_ref.shape[0]
    row_count, share = mine.shape[0], mine.shape[1]
    width = packed_ref.shape[2]
    inner, outer = gathered.shape[:2]
    partner = rank + (1 - 2 * lax.rem(rank, 2)) if inner == 2 else rank

    def remote(source, target, send_sem, recv_sem, axis, index):
        return pltpu.make_async_remote_copy(
            src_ref=source,
            dst_ref=target,
            send_sem=send_sem,
            recv_sem=recv_sem,
            device_id={axis: index},
            device_id_type=pl.DeviceIdType.MESH,
        )

    barrier = pltpu.get_barrier_semaphore()
    for step in range(1, peers):
        pl.semaphore_signal(
            barrier, inc=1, device_id={"blk": lax.rem(rank + step, peers)},
            device_id_type=pl.DeviceIdType.MESH,
        )
    for step in range(1, groups):
        pl.semaphore_signal(
            barrier, inc=1, device_id={"grp": lax.rem(group + step, groups)},
            device_id_type=pl.DeviceIdType.MESH,
        )
    pl.semaphore_wait(barrier, peers + groups - 2)

    firsts, peaks = [], []
    for step in range(1, peers):
        target = lax.rem(rank + step, peers)
        firsts.append(
            remote(
                packed_ref.at[:, pl.ds(pl.multiple_of(target * share, share), share)],
                arrived.at[step], send_one.at[step], recv_one.at[step], "blk", target,
            )
        )
        peaks.append(
            remote(
                peaks_ref, peak_in.at[step], send_peak.at[step], recv_peak.at[step], "blk", target
            )
        )
    for copy in peaks + [firsts[step - 1] for step in far_first(peers)]:
        copy.start()
    arrived[0] = packed_ref[:, pl.ds(pl.multiple_of(rank * share, share), share)]
    top = peaks_ref[...]
    for step, copy in enumerate(peaks, 1):
        copy.wait_recv()
        top = jnp.maximum(top, peak_in[step])
    peak_own[...] = top
    for copy in firsts:
        copy.wait_recv()
    for row in range(row_count):
        place = jnp.int32(0)
        for slot in range(peers * slot_count):
            owner, local = slot // slot_count, slot % slot_count
            match = jnp.logical_and(rows_ref[0, slot] == row, local < counts_ref[0, owner])
            spot = lax.rem(rank - owner + peers, peers) * slot_count + local
            place = jnp.where(match, spot, place)
        mine[row] = arrived[place // slot_count, lax.rem(place, slot_count)]
    seconds, tops = [], []
    for step in range(1, groups):
        tops.append(
            remote(
                peak_own, peak_out.at[step], send_top.at[step], recv_top.at[step],
                "grp", lax.rem(group + step, groups),
            )
        )
    for step in range(1, outer):
        seconds.append(
            remote(
                mine, gathered.at[0, step], send_two.at[step], recv_two.at[step],
                "blk", lax.rem(rank + step * inner, peers),
            )
        )
    thirds = []
    for step in range(outer if inner == 2 else 0):
        thirds.append(
            remote(
                gathered.at[0, step] if step else mine, gathered.at[1, step],
                send_three.at[step], recv_three.at[step], "blk", partner,
            )
        )
    for copy in tops + [seconds[step - 1] for step in far_first(outer)]:
        copy.start()
    if thirds:
        thirds[0].start()
    gathered[0, 0] = mine[...]
    for step in far_first(outer):
        seconds[step - 1].wait_recv()
        if thirds:
            thirds[step].start()
    for step, copy in enumerate(tops, 1):
        copy.wait_recv()
        top = jnp.maximum(top, peak_out[step])
    off_ref[...] = top
    for copy in thirds:
        copy.wait_recv()
    spots = []
    for owner in range(peers):
        side = lax.rem(rank + owner, inner)
        base = rank + side * (partner - rank)
        spots.append((side, lax.rem(base - owner + peers, peers) // inner))
    for row in range(row_count):
        whole = jnp.concatenate([gathered[side, spot, row] for side, spot in spots], axis=0)
        start = 0
        for above in range(4):
            for below in range(above, 4):
                block = whole[start : start + width]
                start += width
                first = slice(above * width, (above + 1) * width)
                second = slice(below * width, (below + 1) * width)
                chosen_ref[row, first, second] = block
                if above != below:
                    chosen_ref[row, second, first] = block.T
    for copy in firsts + peaks + tops + seconds + thirds:
        copy.wait_send()


def exchange(packed, peaks, live_counts, slot_row, row_count, size, peers, groups):
    slot_count, packed_rows, width = packed.shape
    share = packed_rows // peers
    inner = 1 if peers % 2 else 2
    outer = peers // inner
    vmem = pl.BlockSpec(memory_space=pltpu.VMEM)
    smem = pl.BlockSpec(memory_space=pltpu.SMEM)
    dma = pltpu.SemaphoreType.DMA
    return pl.pallas_call(
        functools.partial(exchange_kernel, peers, groups),
        name="exchange",
        out_shape=(
            jax.ShapeDtypeStruct((row_count, size, size), bf16),
            jax.ShapeDtypeStruct(peaks.shape, f32),
        ),
        in_specs=[vmem, vmem, smem, smem],
        out_specs=(vmem, vmem),
        scratch_shapes=[
            pltpu.VMEM((peers, slot_count, share, width), bf16),
            pltpu.VMEM((row_count, share, width), bf16),
            pltpu.VMEM((inner, outer, row_count, share, width), bf16),
            pltpu.VMEM((peers,) + peaks.shape, f32),
            pltpu.VMEM(peaks.shape, f32),
            pltpu.VMEM((groups,) + peaks.shape, f32),
            dma((peers,)), dma((peers,)), dma((outer,)), dma((outer,)), dma((outer,)),
            dma((outer,)), dma((peers,)), dma((peers,)), dma((groups,)), dma((groups,)),
        ],
        compiler_params=pltpu.CompilerParams(
            collective_id=0, has_side_effects=True, vmem_limit_bytes=16 * 1024 * 1024
        ),
        cost_estimate=pl.CostEstimate(
            flops=10**10, bytes_accessed=2 * row_count * size * size, transcendentals=0
        ),
    )(packed, peaks, live_counts, slot_row)


def update_kernel(chosen_ref, grads_ref, updates_ref):
    updates_ref[0, 0] = dot(chosen_ref[0], grads_ref[0, pl.program_id(0)]).astype(bf16)


def update(chosen, gradients):
    row_count, size, columns = gradients.shape[1:]
    height = size // 2
    return pl.pallas_call(
        update_kernel,
        name="update",
        grid=(row_count, 2),
        out_shape=jax.ShapeDtypeStruct(gradients.shape, bf16),
        in_specs=[
            pl.BlockSpec((1, height, size), lambda row, part: (row, part, 0)),
            pl.BlockSpec(memory_space=pltpu.VMEM),
        ],
        out_specs=pl.BlockSpec((1, 1, height, columns), lambda row, part: (0, row, part, 0)),
        compiler_params=pltpu.CompilerParams(vmem_limit_bytes=24 * 1024 * 1024),
        cost_estimate=pl.CostEstimate(
            flops=2 * row_count * size * size * columns,
            bytes_accessed=2 * row_count * size * columns,
            transcendentals=0,
        ),
    )(chosen, gradients)


def per_device(peers, groups, statistics, gradients, live_counts, slot_row, sweeps):
    row_count, size = gradients.shape[1], gradients.shape[2]
    width = size // 4
    share = -(-10 * width // (16 * peers)) * 16
    packed, peaks = jacobi(statistics, live_counts, sweeps, share * peers)
    chosen, top = exchange(
        packed, peaks, live_counts, slot_row, row_count, size, peers, groups
    )
    return (update(chosen, gradients), top[:MAXS, 0])


def solution(mesh):
    in_specs = (
        P("grp", "blk", None, None),
        P("grp", None, None, "blk"),
        P("grp", None),
        P("grp", None),
        P("grp", "blk"),
    )
    out_specs = (P("grp", None, None, "blk"), P())
    return jax.shard_map(
        functools.partial(per_device, mesh.shape["blk"], mesh.shape["grp"]),
        mesh=mesh,
        in_specs=in_specs,
        out_specs=out_specs,
        check_vma=False,
    )
```

profile of v0, /device:TPU:113, one launch (start us, length us, event | category | flops | bytes accessed | tf_op | source)
XLA Modules:
  0.0 157.7 jit_solution(12581220612414903300)
XLA Ops:
  0.6 0.0 copy-start.4
  0.6 1.6 %copy-done.4 = f32[1,2,512,512]{3,2,1,0:T(8,128)S(1)} copy-done((f32[1,2,512,512]{3,2,1,0:T(8,128)S(1)}, f32[1,2,512,512]{3,2,1,0:T(8,128)}, u32[]{:S(2)}) %copy-start.4) | copy-done | bytes 2097176
  2.2 0.0 copy-start.5
  2.2 0.7 copy-done.5
  2.9 0.0 copy-start.6
  2.9 0.7 copy-done.6
  3.5 0.0 copy-start.7
  3.5 34.4 %jacobi.1 = (bf16[2,1536,128]{2,1,0:T(8,128)(2,1)S(1)}, f32[8,128]{1,0:T(8,128)S(1)}) custom-call(f32[1,2,512,512]{3,2,1,0:T(8,128)S(1)} %copy-done.4, s32[1,32]{1,0:T(1,128)S(1)} %copy-done.6, s32[1,2]{1,0:T(1,128)S(1)} %copy-done.5), custom_call_target="tpu_custom_call" | custom-call | flops 10000000000 | bytes 2097152 | tf_op jit(solution)/shard_map/jacobi/pallas_call | solution.py:286
  38.0 0.0 copy-done.7
  38.0 72.6 %exchange.1 = (bf16[16,512,512]{2,1,0:T(8,128)(2,1)S(1)}, f32[8,128]{1,0:T(8,128)S(1)}) custom-call(bf16[2,1536,128]{2,1,0:T(8,128)(2,1)S(1)} %get-tuple-element.6.packed_ref, f32[8,128]{1,0:T(8,128)S(1)} %get-tuple-element.7.peaks_ref, s32[1,32]{1,0:T(1,128)S(1)} %copy-done.6, s32[1,64]{1,0:T(1,128)S(1)} %copy-done.7), custom_call_target="tpu_custom_call" | custom-call | flops 10000000000 | bytes 8388608 | tf_op jit(solution)/shard_map/exchange/pallas_call | solution.py:450
  110.6 0.0 copy-start.2
  110.6 3.2 %copy-done.2 = bf16[16,512,512]{2,1,0:T(8,128)(2,1)} copy-done((bf16[16,512,512]{2,1,0:T(8,128)(2,1)}, bf16[16,512,512]{2,1,0:T(8,128)(2,1)S(1)}, u32[]{:S(2)}) %copy-start.2) | copy-done | bytes 8388632
  113.9 0.6 slice_reduce_fusion
  114.5 11.5 %copy.9.grads_ref = bf16[1,16,512,448]{3,2,1,0:T(8,128)(2,1)} copy(bf16[1,16,512,448]{2,3,1,0:T(8,128)(2,1)} %param.6) | data formatting | bytes 14680064 | tf_op args[1]
  126.0 0.0 copy-start.1
  126.0 3.4 %copy-done.1 = bf16[1,16,512,448]{3,2,1,0:T(8,128)(2,1)S(1)} copy-done((bf16[1,16,512,448]{3,2,1,0:T(8,128)(2,1)S(1)}, bf16[1,16,512,448]{3,2,1,0:T(8,128)(2,1)}, u32[]{:S(2)}) %copy-start.1) | copy-done | bytes 7340056
  129.4 0.0 copy-start.3
  129.4 3.4 %copy-done.3 = bf16[16,512,512]{2,1,0:T(8,128)(2,1)S(1)} copy-done((bf16[16,512,512]{2,1,0:T(8,128)(2,1)S(1)}, bf16[16,512,512]{2,1,0:T(8,128)(2,1)}, u32[]{:S(2)}) %copy-start.3) | copy-done | bytes 8388632
  132.8 9.8 %update.1 = bf16[1,16,512,448]{3,2,1,0:T(8,128)(2,1)S(1)} custom-call(bf16[16,512,512]{2,1,0:T(8,128)(2,1)S(1)} %copy-done.3, bf16[1,16,512,448]{3,2,1,0:T(8,128)(2,1)S(1)} %copy-done.1), custom_call_target="tpu_custom_call" | custom-call | flops 3758096384 | bytes 7340032 | tf_op jit(solution)/shard_map/update/pallas_call | solution.py:485
  142.5 0.0 copy-start
  142.6 3.2 %copy-done = bf16[1,16,512,448]{3,2,1,0:T(8,128)(2,1)} copy-done((bf16[1,16,512,448]{3,2,1,0:T(8,128)(2,1)}, bf16[1,16,512,448]{3,2,1,0:T(8,128)(2,1)S(1)}, u32[]{:S(2)}) %copy-start) | copy-done | bytes 7340056
  145.8 11.9 %copy.10 = bf16[1,16,512,448]{2,3,1,0:T(8,128)(2,1)} copy(bf16[1,16,512,448]{3,2,1,0:T(8,128)(2,1)} %copy-done) | data formatting | bytes 14680064
Async XLA Ops:
  0.6 1.6 %copy-start.4 = (f32[1,2,512,512]{3,2,1,0:T(8,128)S(1)}, f32[1,2,512,512]{3,2,1,0:T(8,128)}, u32[]{:S(2)}) copy-start(f32[1,2,512,512]{3,2,1,0:T(8,128)} %stats_ref.1) | copy-start | bytes 6291460
  2.2 0.7 copy-start.5
  2.9 0.7 copy-start.6
  3.5 34.4 %copy-start.7 = (s32[1,64]{1,0:T(1,128)S(1)}, s32[1,64]{1,0:T(1,128)}, u32[]{:S(2)}) copy-start(s32[1,64]{1,0:T(1,128)} %rows_ref.1) | copy-start | bytes 772
  110.6 3.2 %copy-start.2 = (bf16[16,512,512]{2,1,0:T(8,128)(2,1)}, bf16[16,512,512]{2,1,0:T(8,128)(2,1)S(1)}, u32[]{:S(2)}) copy-start(bf16[16,512,512]{2,1,0:T(8,128)(2,1)S(1)} %get-tuple-element.8.chosen_ref) | copy-start | bytes 25165828
  126.0 3.4 %copy-start.1 = (bf16[1,16,512,448]{3,2,1,0:T(8,128)(2,1)S(1)}, bf16[1,16,512,448]{3,2,1,0:T(8,128)(2,1)}, u32[]{:S(2)}) copy-start(bf16[1,16,512,448]{3,2,1,0:T(8,128)(2,1)} %copy.9.grads_ref) | copy-start | bytes 22020100
  129.4 3.4 %copy-start.3 = (bf16[16,512,512]{2,1,0:T(8,128)(2,1)S(1)}, bf16[16,512,512]{2,1,0:T(8,128)(2,1)}, u32[]{:S(2)}) copy-start(bf16[16,512,512]{2,1,0:T(8,128)(2,1)} %copy-done.2) | copy-start | bytes 25165828
  142.5 3.2 %copy-start = (bf16[1,16,512,448]{3,2,1,0:T(8,128)(2,1)}, bf16[1,16,512,448]{3,2,1,0:T(8,128)(2,1)S(1)}, u32[]{:S(2)}) copy-start(bf16[1,16,512,448]{3,2,1,0:T(8,128)(2,1)S(1)} %update.1) | copy-start | bytes 22020100
where the time goes:
time: 160 us; the launch traced here: 158 us
  Pallas kernels  117 us (73%)
  local copies, waits for them, and re-layouts  40.2 us (25%)
    pallas_call x1, Pallas kernels, exchange(): pl.pallas_call(functools.partial(exchange_kernel, peers, groups), name='e...  72.6 us
    unnamed x18, local copies, waits for them, and re-layouts  39.6 us
    pallas_call x1, Pallas kernels, jacobi(): pl.pallas_call(jacobi_kernel, name='jacobi', out_shape=(jax.ShapeDtypeStr...  34.4 us
    pallas_call x1, Pallas kernels, update(): pl.pallas_call(update_kernel, name='update', grid=(row_count, 2), out_sha...  9.75 us

commit v1 on v0

--- a/solution.py
+++ b/solution.py
@@ -476,23 +476,20 @@
 
 
 def update_kernel(chosen_ref, grads_ref, updates_ref):
-    updates_ref[0, 0] = dot(chosen_ref[0], grads_ref[0, pl.program_id(0)]).astype(bf16)
+    updates_ref[0, 0] = dot(grads_ref[0, 0], chosen_ref[0]).astype(bf16)
 
 
 def update(chosen, gradients):
-    row_count, size, columns = gradients.shape[1:]
-    height = size // 2
+    row_count, columns, size = gradients.shape[1:]
+    block = pl.BlockSpec((1, 1, columns, size), lambda row: (0, row, 0, 0))
     return pl.pallas_call(
         update_kernel,
         name="update",
-        grid=(row_count, 2),
+        grid=(row_count,),
         out_shape=jax.ShapeDtypeStruct(gradients.shape, bf16),
-        in_specs=[
-            pl.BlockSpec((1, height, size), lambda row, part: (row, part, 0)),
-            pl.BlockSpec(memory_space=pltpu.VMEM),
-        ],
-        out_specs=pl.BlockSpec((1, 1, height, columns), lambda row, part: (0, row, part, 0)),
-        compiler_params=pltpu.CompilerParams(vmem_limit_bytes=24 * 1024 * 1024),
+        in_specs=[pl.BlockSpec((1, size, size), lambda row: (row, 0, 0)), block],
+        out_specs=block,
+        compiler_params=pltpu.CompilerParams(vmem_limit_bytes=16 * 1024 * 1024),
         cost_estimate=pl.CostEstimate(
             flops=2 * row_count * size * size * columns,
             bytes_accessed=2 * row_count * size * columns,
@@ -509,7 +506,8 @@
     chosen, top = exchange(
         packed, peaks, live_counts, slot_row, row_count, size, peers, groups
     )
-    return (update(chosen, gradients), top[:MAXS, 0])
+    updates = update(chosen, jnp.swapaxes(gradients, 2, 3))
+    return (jnp.swapaxes(updates, 2, 3), top[:MAXS, 0])
 
 
 def solution(mesh):

time: 160 us -> 133 us (0.83)
  the two profiles are of different devices: /device:TPU:113 before, /device:TPU:1 now
where the time goes in v1:
time: 133 us; the launch traced here: 131 us
  Pallas kernels  127 us (95%)
  local copies, waits for them, and re-layouts  3.53 us (3%)
    pallas_call x1, Pallas kernels, exchange(): pl.pallas_call(functools.partial(exchange_kernel, peers, groups), name='e...  89.2 us
    pallas_call x1, Pallas kernels, jacobi(): pl.pallas_call(jacobi_kernel, name='jacobi', out_shape=(jax.ShapeDtypeStr...  28.2 us
    pallas_call x1, Pallas kernels, update(): pl.pallas_call(update_kernel, name='update', grid=(row_count,), out_shape...  9.81 us
    unnamed x12, local copies, waits for them, and re-layouts  2.91 us

profile of v1, /device:TPU:1, one launch (start us, length us, event | category | flops | bytes accessed | tf_op | source)
XLA Modules:
  0.0 131.5 jit_solution(6505914327094521895)
XLA Ops:
  0.6 0.0 copy-start
  0.6 1.6 %copy-done = f32[1,2,512,512]{3,2,1,0:T(8,128)S(1)} copy-done((f32[1,2,512,512]{3,2,1,0:T(8,128)S(1)}, f32[1,2,512,512]{3,2,1,0:T(8,128)}, u32[]{:S(2)}) %copy-start) | copy-done | bytes 2097176
  2.2 0.0 copy-start.1
  2.2 0.7 copy-done.1
  2.9 0.0 copy-start.2
  2.9 0.7 copy-done.2
  3.5 0.0 copy-start.3
  3.5 0.0 slice-start
  3.5 28.2 %jacobi.1 = (bf16[2,1536,128]{2,1,0:T(8,128)(2,1)S(1)}, f32[8,128]{1,0:T(8,128)S(1)}) custom-call(f32[1,2,512,512]{3,2,1,0:T(8,128)S(1)} %copy-done, s32[1,32]{1,0:T(1,128)S(1)} %copy-done.2, s32[1,2]{1,0:T(1,128)S(1)} %copy-done.1), custom_call_target="tpu_custom_call" | custom-call | flops 10000000000 | bytes 2097152 | tf_op jit(solution)/shard_map/jacobi/pallas_call | solution.py:286
  31.8 0.0 slice-start.1
  31.8 0.0 copy-done.3
  31.8 89.2 %exchange.1 = (bf16[16,512,512]{2,1,0:T(8,128)(2,1)S(1)}, f32[8,128]{1,0:T(8,128)S(1)}) custom-call(bf16[2,1536,128]{2,1,0:T(8,128)(2,1)S(1)} %get-tuple-element.6.packed_ref, f32[8,128]{1,0:T(8,128)S(1)} %get-tuple-element.7.peaks_ref, s32[1,32]{1,0:T(1,128)S(1)} %copy-done.2, s32[1,64]{1,0:T(1,128)S(1)} %copy-done.3), custom_call_target="tpu_custom_call" | custom-call | flops 10000000000 | bytes 8388608 | tf_op jit(solution)/shard_map/exchange/pallas_call | solution.py:450
  121.0 0.0 slice-done
  121.0 0.0 slice-done.1
  121.0 9.8 %update.1 = bf16[1,16,448,512]{3,2,1,0:T(8,128)(2,1)} custom-call(bf16[16,512,512]{2,1,0:T(8,128)(2,1)S(1)} %get-tuple-element.8.chosen_ref, bf16[1,16,448,512]{3,2,1,0:T(8,128)(2,1)S(1)} %bitcast.4), custom_call_target="tpu_custom_call" | custom-call | flops 3758096384 | bytes 7340032 | tf_op jit(solution)/shard_map/update/pallas_call | solution.py:485
  130.9 0.6 slice_reduce_fusion
  (1 shorter events, 0.0 us)
Async XLA Ops:
  0.6 1.6 %copy-start = (f32[1,2,512,512]{3,2,1,0:T(8,128)S(1)}, f32[1,2,512,512]{3,2,1,0:T(8,128)}, u32[]{:S(2)}) copy-start(f32[1,2,512,512]{3,2,1,0:T(8,128)} %stats_ref.1) | copy-start | bytes 6291460
  2.2 0.7 copy-start.1
  2.9 0.7 copy-start.2
  3.5 28.2 %copy-start.3 = (s32[1,64]{1,0:T(1,128)S(1)}, s32[1,64]{1,0:T(1,128)}, u32[]{:S(2)}) copy-start(s32[1,64]{1,0:T(1,128)} %rows_ref.1) | copy-start | bytes 772
  3.5 117.5 %slice-start = ((s8[7340032]{0:T(1024)(128)(4,1)}), s8[4194304]{0:T(1024)(128)(4,1)S(1)}, s32[]{:S(2)}) async-start(s8[7340032]{0:T(1024)(128)(4,1)} %bitcast.2), calls=%async_computation | async-start | bytes 8388608
  31.8 89.3 %slice-start.1 = ((s8[7340032]{0:T(1024)(128)(4,1)}), s8[3145728]{0:T(1024)(128)(4,1)S(1)}, s32[]{:S(2)}) async-start(s8[7340032]{0:T(1024)(128)(4,1)} %bitcast.2), calls=%async_computation.1 | async-start | bytes 6291456

commit v2 on v1

--- a/solution.py
+++ b/solution.py
@@ -205,7 +205,6 @@
         off_ref[row, :] = jnp.maximum(off_ref[row, :], norm)
 
     off_ref[...] = jnp.zeros_like(off_ref)
-    packed_ref[...] = jnp.zeros_like(packed_ref)
     ident_rows = jnp.where(eye_mask(size), 1.0, 0.0).astype(bf16)
 
     for slot in range(slot_count):
@@ -288,7 +287,7 @@
         name="jacobi",
         out_shape=(
             jax.ShapeDtypeStruct((slot_count, packed_rows, width), bf16),
-            jax.ShapeDtypeStruct((8, width), f32),
+            jax.ShapeDtypeStruct((MAXS, width), f32),
         ),
         in_specs=[vmem, smem, smem],
         out_specs=(vmem, vmem),
@@ -308,22 +307,20 @@
     )(statistics, live_counts, sweeps)
 
 
-def far_first(count):
-    return sorted(range(1, count), key=lambda step: abs(2 * step - count))
-
-
 def exchange_kernel(
-    peers, groups, packed_ref, peaks_ref, counts_ref, rows_ref, chosen_ref, off_ref,
-    arrived, mine, gathered, peak_in, peak_own, peak_out,
-    send_one, recv_one, send_two, recv_two, send_three, recv_three, send_peak, recv_peak, send_top, recv_top,
+    side, groups, packed_ref, peaks_ref, counts_ref, rows_ref, whole_ref, off_ref,
+    arrived, mine, peak_in, peak_own, peak_out,
+    send_one, recv_one, send_two, recv_two, send_near, recv_near, send_peak, recv_peak, send_top, recv_top,
 ):
+    chips = side * side
+    peers = 2 * chips
     rank = lax.axis_index("blk")
     group = lax.axis_index("grp")
     slot_count = packed_ref.shape[0]
     row_count, share = mine.shape[0], mine.shape[1]
-    width = packed_ref.shape[2]
-    inner, outer = gathered.shape[:2]
-    partner = rank + (1 - 2 * lax.rem(rank, 2)) if inner == 2 else rank
+    core = lax.rem(rank, 2)
+    place_x, place_z = rank // (2 * side), lax.rem(rank // 2, side)
+    partner = rank + 1 - 2 * core
 
     def remote(source, target, send_sem, recv_sem, axis, index):
         return pltpu.make_async_remote_copy(
@@ -348,13 +345,17 @@
         )
     pl.semaphore_wait(barrier, peers + groups - 2)
 
+    def strip(index):
+        return pl.ds(pl.multiple_of(index * share, share), share)
+
     firsts, peaks = [], []
+    own_slots = pl.ds(rank * slot_count, slot_count)
     for step in range(1, peers):
         target = lax.rem(rank + step, peers)
         firsts.append(
             remote(
-                packed_ref.at[:, pl.ds(pl.multiple_of(target * share, share), share)],
-                arrived.at[step], send_one.at[step], recv_one.at[step], "blk", target,
+                packed_ref.at[:, strip(target)],
+                arrived.at[own_slots], send_one.at[step], recv_one.at[step], "blk", target,
             )
         )
         peaks.append(
@@ -362,25 +363,122 @@
                 peaks_ref, peak_in.at[step], send_peak.at[step], recv_peak.at[step], "blk", target
             )
         )
-    for copy in peaks + [firsts[step - 1] for step in far_first(peers)]:
+    for copy in firsts + peaks:
         copy.start()
-    arrived[0] = packed_ref[:, pl.ds(pl.multiple_of(rank * share, share), share)]
+    for local in range(slot_count):
+        arrived[rank * slot_count + local] = packed_ref[local, strip(rank)]
+
+    def find(slot, places):
+        live = lax.rem(slot, slot_count) < counts_ref[0, slot // slot_count]
+        wanted = jnp.where(live, rows_ref[0, slot], -1)
+        return tuple(
+            jnp.where(wanted == row, slot, place) for row, place in enumerate(places)
+        )
+
+    places = lax.fori_loop(
+        0, peers * slot_count, find, tuple(jnp.int32(0) for _ in range(row_count))
+    )
+    for copy in firsts:
+        copy.wait_recv()
+    for row in range(row_count):
+        mine[row] = arrived[places[row]]
+
+    half = row_count // 2
+    quarter = half // 2
+
+    def rank_of(order, along, across):
+        x, z = (across, along) if order == 0 else (along, across)
+        return (lax.rem(x + side, side) * side + lax.rem(z + side, side)) * 2 + core
+
+    started = []
+
+    class Route:
+        def __init__(self, order):
+            self.order = order
+            self.at = (place_z, place_x) if order == 0 else (place_x, place_z)
+            self.base = order * half
+            self.counter = 0
+
+        def source(self, hop_one, hop_two):
+            return rank_of(self.order, self.at[0] + hop_one, self.at[1] + hop_two)
+
+        def neighbour(self, axis, move):
+            return self.source(move, 0) if axis == 0 else self.source(0, move)
+
+        def rows(self, part):
+            if part is None:
+                return pl.ds(self.base, half)
+            return pl.ds(self.base + part * quarter, quarter)
+
+        def copy(self, slot, hop_one, hop_two, part, axis, move):
+            at = self.source(hop_one, hop_two)
+            rows = self.rows(part)
+            if hop_one == 0 and hop_two == 0:
+                source = mine.at[rows]
+            else:
+                source = whole_ref.at[rows, strip(at)]
+            index = 20 * self.order + slot
+            return remote(
+                source, whole_ref.at[rows, strip(at)],
+                send_two.at[index], recv_two.at[index], "blk", self.neighbour(axis, move),
+            )
+
+    near = {}
+
+    def share_near(route, hop_one, hop_two):
+        at = route.source(hop_one, hop_two)
+        rows = route.rows(None)
+        own = hop_one == 0 and hop_two == 0
+        source = mine.at[rows] if own else whole_ref.at[rows, strip(at)]
+        index = 16 * route.order + 4 * (hop_one + 1) + (hop_two + 1)
+        copy = remote(
+            source, whole_ref.at[rows, strip(at)],
+            send_near.at[index], recv_near.at[index], "blk", partner,
+        )
+        copy.start()
+        near[index] = copy
+
+    routes = (Route(0), Route(1))
+    sends = {}
+
+    def launch(route, slot, hop_one, hop_two, part, axis, move):
+        copy = route.copy(slot, hop_one, hop_two, part, axis, move)
+        copy.start()
+        sends[route.order, slot] = copy
+
+    def arrive(route, slot):
+        sends[route.order, slot].wait_recv()
+
+    def spread(route, hop_one):
+        slot = 4 + 4 * (hop_one + 1)
+        launch(route, slot, hop_one, 0, None, 1, 1)
+        launch(route, slot + 1, hop_one, 0, None, 1, -1)
+        share_near(route, hop_one, 0)
+
+    def along(route, move):
+        arrive(route, 0 if move < 0 else 1)
+        launch(route, 2 if move < 0 else 3, move, 0, 0 if move < 0 else 1, 0, -move)
+
+    def across(route, hop_one, move):
+        slot = 4 + 4 * (hop_one + 1)
+        arrive(route, slot if move < 0 else slot + 1)
+        launch(
+            route, slot + (2 if move < 0 else 3), hop_one, move, 0 if move < 0 else 1, 1, -move
+        )
+        share_near(route, hop_one, move)
+
+    for route in routes:
+        launch(route, 0, 0, 0, None, 0, 1)
+        launch(route, 1, 0, 0, None, 0, -1)
+    for route in routes:
+        spread(route, 0)
+    whole_ref[:, strip(rank)] = mine[...]
     top = peaks_ref[...]
     for step, copy in enumerate(peaks, 1):
         copy.wait_recv()
         top = jnp.maximum(top, peak_in[step])
     peak_own[...] = top
-    for copy in firsts:
-        copy.wait_recv()
-    for row in range(row_count):
-        place = jnp.int32(0)
-        for slot in range(peers * slot_count):
-            owner, local = slot // slot_count, slot % slot_count
-            match = jnp.logical_and(rows_ref[0, slot] == row, local < counts_ref[0, owner])
-            spot = lax.rem(rank - owner + peers, peers) * slot_count + local
-            place = jnp.where(match, spot, place)
-        mine[row] = arrived[place // slot_count, lax.rem(place, slot_count)]
-    seconds, tops = [], []
+    tops = []
     for step in range(1, groups):
         tops.append(
             remote(
@@ -388,126 +486,125 @@
                 "grp", lax.rem(group + step, groups),
             )
         )
-    for step in range(1, outer):
-        seconds.append(
-            remote(
-                mine, gathered.at[0, step], send_two.at[step], recv_two.at[step],
-                "blk", lax.rem(rank + step * inner, peers),
-            )
-        )
-    thirds = []
-    for step in range(outer if inner == 2 else 0):
-        thirds.append(
-            remote(
-                gathered.at[0, step] if step else mine, gathered.at[1, step],
-                send_three.at[step], recv_three.at[step], "blk", partner,
-            )
-        )
-    for copy in tops + [seconds[step - 1] for step in far_first(outer)]:
+    for copy in tops:
         copy.start()
-    if thirds:
-        thirds[0].start()
-    gathered[0, 0] = mine[...]
-    for step in far_first(outer):
-        seconds[step - 1].wait_recv()
-        if thirds:
-            thirds[step].start()
+    for move in (-1, 1):
+        for route in routes:
+            along(route, move)
+        for route in routes:
+            spread(route, move)
+    for move in (-1, 1):
+        for route in routes:
+            across(route, 0, move)
+    for route in routes:
+        arrive(route, 2)
+        arrive(route, 3)
+        spread(route, 2)
     for step, copy in enumerate(tops, 1):
         copy.wait_recv()
         top = jnp.maximum(top, peak_out[step])
     off_ref[...] = top
-    for copy in thirds:
+    for hop_one in (-1, 1, 2):
+        for move in (-1, 1):
+            for route in routes:
+                across(route, hop_one, move)
+    for hop_one in (0, -1, 1, 2):
+        for route in routes:
+            slot = 4 + 4 * (hop_one + 1)
+            arrive(route, slot + 2)
+            arrive(route, slot + 3)
+            share_near(route, hop_one, 2)
+    for copy in near.values():
         copy.wait_recv()
-    spots = []
-    for owner in range(peers):
-        side = lax.rem(rank + owner, inner)
-        base = rank + side * (partner - rank)
-        spots.append((side, lax.rem(base - owner + peers, peers) // inner))
-    for row in range(row_count):
-        whole = jnp.concatenate([gathered[side, spot, row] for side, spot in spots], axis=0)
-        start = 0
-        for above in range(4):
-            for below in range(above, 4):
-                block = whole[start : start + width]
-                start += width
-                first = slice(above * width, (above + 1) * width)
-                second = slice(below * width, (below + 1) * width)
-                chosen_ref[row, first, second] = block
-                if above != below:
-                    chosen_ref[row, second, first] = block.T
-    for copy in firsts + peaks + tops + seconds + thirds:
+    for copy in firsts + peaks + tops + list(sends.values()) + list(near.values()):
         copy.wait_send()
 
 
-def exchange(packed, peaks, live_counts, slot_row, row_count, size, peers, groups):
+def exchange(packed, peaks, live_counts, slot_row, row_count, side, groups):
     slot_count, packed_rows, width = packed.shape
+    chips = side * side
+    peers = 2 * chips
     share = packed_rows // peers
-    inner = 1 if peers % 2 else 2
-    outer = peers // inner
     vmem = pl.BlockSpec(memory_space=pltpu.VMEM)
     smem = pl.BlockSpec(memory_space=pltpu.SMEM)
     dma = pltpu.SemaphoreType.DMA
     return pl.pallas_call(
-        functools.partial(exchange_kernel, peers, groups),
+        functools.partial(exchange_kernel, side, groups),
         name="exchange",
         out_shape=(
-            jax.ShapeDtypeStruct((row_count, size, size), bf16),
+            jax.ShapeDtypeStruct((row_count, packed_rows, width), bf16),
             jax.ShapeDtypeStruct(peaks.shape, f32),
         ),
         in_specs=[vmem, vmem, smem, smem],
         out_specs=(vmem, vmem),
         scratch_shapes=[
-            pltpu.VMEM((peers, slot_count, share, width), bf16),
+            pltpu.VMEM((peers * slot_count, share, width), bf16),
             pltpu.VMEM((row_count, share, width), bf16),
-            pltpu.VMEM((inner, outer, row_count, share, width), bf16),
             pltpu.VMEM((peers,) + peaks.shape, f32),
             pltpu.VMEM(peaks.shape, f32),
             pltpu.VMEM((groups,) + peaks.shape, f32),
-            dma((peers,)), dma((peers,)), dma((outer,)), dma((outer,)), dma((outer,)),
-            dma((outer,)), dma((peers,)), dma((peers,)), dma((groups,)), dma((groups,)),
+            dma((peers,)), dma((peers,)), dma((40,)), dma((40,)), dma((32,)),
+            dma((32,)), dma((peers,)), dma((peers,)), dma((groups,)), dma((groups,)),
         ],
         compiler_params=pltpu.CompilerParams(
             collective_id=0, has_side_effects=True, vmem_limit_bytes=16 * 1024 * 1024
         ),
         cost_estimate=pl.CostEstimate(
-            flops=10**10, bytes_accessed=2 * row_count * size * size, transcendentals=0
+            flops=10**10, bytes_accessed=2 * row_count * packed_rows * width, transcendentals=0
         ),
     )(packed, peaks, live_counts, slot_row)
 
 
-def update_kernel(chosen_ref, grads_ref, updates_ref):
-    updates_ref[0, 0] = dot(grads_ref[0, 0], chosen_ref[0]).astype(bf16)
-
-
-def update(chosen, gradients):
+def update_kernel(whole_ref, grads_ref, updates_ref):
+    width = whole_ref.shape[2]
+    for row in range(whole_ref.shape[0]):
+        blocks = {}
+        start = 0
+        for above in range(4):
+            for below in range(above, 4):
+                block = whole_ref[row, start : start + width]
+                start += width
+                blocks[above, below] = block
+                if above != below:
+                    blocks[below, above] = block.T
+        factor = jnp.concatenate(
+            [
+                jnp.concatenate([blocks[above, below] for below in range(4)], axis=1)
+                for above in range(4)
+            ],
+            axis=0,
+        )
+        updates_ref[0, row] = dot(grads_ref[0, row], factor).astype(bf16)
+
+
+def update(whole, gradients):
     row_count, columns, size = gradients.shape[1:]
-    block = pl.BlockSpec((1, 1, columns, size), lambda row: (0, row, 0, 0))
+    rows = 2
+    block = pl.BlockSpec((1, rows, columns, size), lambda row: (0, row, 0, 0))
     return pl.pallas_call(
         update_kernel,
         name="update",
-        grid=(row_count,),
+        grid=(row_count // rows,),
         out_shape=jax.ShapeDtypeStruct(gradients.shape, bf16),
-        in_specs=[pl.BlockSpec((1, size, size), lambda row: (row, 0, 0)), block],
+        in_specs=[pl.BlockSpec((rows,) + whole.shape[1:], lambda row: (row, 0, 0)), block],
         out_specs=block,
-        compiler_params=pltpu.CompilerParams(vmem_limit_bytes=16 * 1024 * 1024),
+        compiler_params=pltpu.CompilerParams(vmem_limit_bytes=24 * 1024 * 1024),
         cost_estimate=pl.CostEstimate(
             flops=2 * row_count * size * size * columns,
             bytes_accessed=2 * row_count * size * columns,
             transcendentals=0,
         ),
-    )(chosen, gradients)
+    )(whole, gradients)
 
 
 def per_device(peers, groups, statistics, gradients, live_counts, slot_row, sweeps):
     row_count, size = gradients.shape[1], gradients.shape[2]
     width = size // 4
-    share = -(-10 * width // (16 * peers)) * 16
-    packed, peaks = jacobi(statistics, live_counts, sweeps, share * peers)
-    chosen, top = exchange(
-        packed, peaks, live_counts, slot_row, row_count, size, peers, groups
-    )
-    updates = update(chosen, jnp.swapaxes(gradients, 2, 3))
-    return (jnp.swapaxes(updates, 2, 3), top[:MAXS, 0])
+    side = next(edge for edge in range(1, peers) if 2 * edge * edge == peers)
+    packed, peaks = jacobi(statistics, live_counts, sweeps, 10 * width)
+    whole, top = exchange(packed, peaks, live_counts, slot_row, row_count, side, groups)
+    updates = update(whole, jnp.swapaxes(gradients, 2, 3))
+    return (jnp.swapaxes(updates, 2, 3), top[:, 0])
 
 
 def solution(mesh):

time: 133 us -> 96.7 us (0.73); the launches traced: 131 us -> 97 us
  Pallas kernels: 127 us -> 92.8 us
    pallas_call x2, Pallas kernels: 99 us -> 48.1 us  [the longest x1 41 us: exchange(): pl.pallas_call(functools.partial(exchange_kernel, side, groups), name='ex...]
    pallas_call x1, Pallas kernels: 28.2 us -> 44.7 us  [jacobi(): pl.pallas_call(jacobi_kernel, name='jacobi', out_shape=(jax.ShapeDtypeStr...]
    unnamed x12 -> x14, local copies, waits for them, and re-layouts: 2.91 us -> 2.91 us
where the time goes in v2:
time: 96.7 us; the launch traced here: 97 us
  Pallas kernels  92.8 us (96%)
  local copies, waits for them, and re-layouts  3.54 us (4%)
    pallas_call x1, Pallas kernels, jacobi(): pl.pallas_call(jacobi_kernel, name='jacobi', out_shape=(jax.ShapeDtypeStr...  44.7 us
    pallas_call x1, Pallas kernels, exchange(): pl.pallas_call(functools.partial(exchange_kernel, side, groups), name='ex...  41 us
    pallas_call x1, Pallas kernels, update(): pl.pallas_call(update_kernel, name='update', grid=(row_count // rows,), o...  7.05 us
    unnamed x14, local copies, waits for them, and re-layouts  2.91 us

profile of v2, /device:TPU:1, one launch (start us, length us, event | category | flops | bytes accessed | tf_op | source)
XLA Modules:
  0.0 97.0 jit_solution(6668378339580088293)
XLA Ops:
  0.6 0.0 copy-start
  0.6 1.6 %copy-done = f32[1,2,512,512]{3,2,1,0:T(8,128)S(1)} copy-done((f32[1,2,512,512]{3,2,1,0:T(8,128)S(1)}, f32[1,2,512,512]{3,2,1,0:T(8,128)}, u32[]{:S(2)}) %copy-start) | copy-done | bytes 2097176
  2.2 0.0 copy-start.1
  2.2 0.7 copy-done.1
  2.9 0.0 copy-start.2
  2.9 0.7 copy-done.2
  3.5 0.0 copy-start.3
  3.5 0.0 copy-start.4
  3.5 0.0 slice-start
  3.5 44.7 %jacobi.1 = (bf16[2,1280,128]{2,1,0:T(8,128)(2,1)S(1)}, f32[2,128]{1,0:T(2,128)S(1)}) custom-call(f32[1,2,512,512]{3,2,1,0:T(8,128)S(1)} %copy-done, s32[1,32]{1,0:T(1,128)S(1)} %copy-done.2, s32[1,2]{1,0:T(1,128)S(1)} %copy-done.1), custom_call_target="tpu_custom_call" | custom-call | flops 10000000000 | bytes 2097152 | tf_op jit(solution)/shard_map/jacobi/pallas_call | solution.py:285
  48.3 0.0 copy-done.3
  48.3 0.0 copy-done.4
  48.3 0.0 slice-start.1
  48.3 41.0 %exchange.1 = (bf16[16,1280,128]{2,1,0:T(8,128)(2,1)S(1)}, f32[2,128]{1,0:T(2,128)S(1)}) custom-call(bf16[2,1280,128]{2,1,0:T(8,128)(2,1)S(1)} %get-tuple-element.6.packed_ref, f32[2,128]{1,0:T(2,128)S(1)} %get-tuple-element.7.peaks_ref, s32[1,32]{1,0:T(1,128)S(1)} %copy-done.3, s32[1,64]{1,0:T(1,128)S(1)} %copy-done.4), custom_call_target="tpu_custom_call" | custom-call | flops 10000000000 | bytes 5242880 | tf_op jit(solution)/shard_map/exchange/pallas_call | solution.py:531
  89.4 0.6 slice_reduce_fusion
  90.0 0.0 slice-done
  90.0 0.0 slice-done.1
  90.0 7.1 %update.1 = bf16[1,16,448,512]{3,2,1,0:T(8,128)(2,1)} custom-call(bf16[16,1280,128]{2,1,0:T(8,128)(2,1)S(1)} %get-tuple-element.8.whole_ref, bf16[1,16,448,512]{3,2,1,0:T(8,128)(2,1)S(1)} %bitcast.4), custom_call_target="tpu_custom_call" | custom-call | flops 3758096384 | bytes 7340032 | tf_op jit(solution)/shard_map/update/pallas_call | solution.py:584
  (1 shorter events, 0.0 us)
Async XLA Ops:
  0.6 1.6 %copy-start = (f32[1,2,512,512]{3,2,1,0:T(8,128)S(1)}, f32[1,2,512,512]{3,2,1,0:T(8,128)}, u32[]{:S(2)}) copy-start(f32[1,2,512,512]{3,2,1,0:T(8,128)} %stats_ref.1) | copy-start | bytes 6291460
  2.2 0.7 copy-start.1
  2.9 0.7 copy-start.2
  3.5 44.7 %copy-start.3 = (s32[1,32]{1,0:T(1,128)S(1)}, s32[1,32]{1,0:T(1,128)}, u32[]{:S(2)}) copy-start(s32[1,32]{1,0:T(1,128)} %counts_ref.3) | copy-start | bytes 388
  3.5 44.7 %copy-start.4 = (s32[1,64]{1,0:T(1,128)S(1)}, s32[1,64]{1,0:T(1,128)}, u32[]{:S(2)}) copy-start(s32[1,64]{1,0:T(1,128)} %rows_ref.1) | copy-start | bytes 772
  3.5 86.4 %slice-start = ((s8[7340032]{0:T(1024)(128)(4,1)}), s8[4194304]{0:T(1024)(128)(4,1)S(1)}, s32[]{:S(2)}) async-start(s8[7340032]{0:T(1024)(128)(4,1)} %bitcast.2), calls=%async_computation | async-start | bytes 8388608
  48.3 41.7 %slice-start.1 = ((s8[7340032]{0:T(1024)(128)(4,1)}), s8[3145728]{0:T(1024)(128)(4,1)S(1)}, s32[]{:S(2)}) async-start(s8[7340032]{0:T(1024)(128)(4,1)} %bitcast.2), calls=%async_computation.1 | async-start | bytes 6291456

commit v3 on v2

--- a/solution.py
+++ b/solution.py
@@ -55,7 +55,7 @@
 
 def jacobi_kernel(
     stats_ref, counts_ref, sweeps_ref, packed_ref, off_ref,
-    mat, vec_high, vec_low, mid_high, mid_low, angle, powers,
+    mat, vec_high, vec_low, mid_high, mid_low, angle, powers, turn,
 ):
     slot_count, size, _ = mat.shape
     width = size // 4
@@ -67,9 +67,31 @@
     def span(member):
         return pl.ds(member * width, width)
 
-    def one_round(slots, pairing):
+    def turn_half(slot, half, pairing):
+        members = pairing[2 * half : 2 * half + 2]
+        columns = tuple(
+            jnp.concatenate([ref[slot, :, span(member)] for member in members], axis=1)
+            for ref in (vec_high, vec_low)
+        )
+        turned = split(dot(left_parts(columns), turn[slot, half]))
+        for place, member in enumerate(members):
+            inner = slice(place * width, (place + 1) * width)
+            vec_high[slot, :, span(member)] = turned[0][:, inner]
+            vec_low[slot, :, span(member)] = turned[1][:, inner]
+
+    def one_round(slots, pairing, before):
         pairs = (pairing[:2], pairing[2:])
         chains = [(at, slot, half) for at, slot in enumerate(slots) for half in range(2)]
+        waiting = [(slot, half) for slot in slots for half in range(2)] if before else []
+        waiting = {
+            point: waiting[point * len(waiting) // 4 : (point + 1) * len(waiting) // 4]
+            for point in range(4)
+        }
+
+        def fill(point):
+            for slot, half in waiting[point]:
+                turn_half(slot, half, before)
+
         outers = []
         peak = jnp.zeros((1, width), f32)
         for at, slot, half in chains:
@@ -84,6 +106,7 @@
             outer = dot3(angles, angles.T)
             outers.append(outer)
             peak = jnp.maximum(peak, jnp.sum(jnp.abs(outer), axis=0, keepdims=True))
+        fill(0)
         kappa = 1.0 + 0.26 * jnp.max(peak)
         count = jnp.int32(0)
         for bound in kappa_steps:
@@ -93,6 +116,7 @@
             error = (1.0 - scale) * identity - (0.25 * scale) * outers[2 * at + half]
             powers[2 * at + half, :, :width] = scale * (identity + error)
             powers[2 * at + half, :, width:] = dot3(error, error)
+        fill(1)
 
         def double(step, carry):
             for at, slot, half in chains:
@@ -107,21 +131,28 @@
 
         lax.fori_loop(0, count, double, 0)
 
+        inverses = []
+        for at, slot, half in chains:
+            inverse = powers[2 * at + half, :, :width]
+            inverses.append(
+                inverse
+                + dot(inverse.astype(bf16), powers[2 * at + half, :, width:].astype(bf16))
+            )
+        fill(2)
+        rights = [
+            dot3(inverses[2 * at + half], angle[2 * at + half]) for at, slot, half in chains
+        ]
+        fill(3)
+        lows = [
+            identity - 0.5 * dot3(angle[2 * at + half].T, rights[2 * at + half])
+            for at, slot, half in chains
+        ]
         flips = {}
         for at, slot, half in chains:
-            first, second = pairs[half]
-            angles = angle[2 * at + half]
-            inverse = powers[2 * at + half, :, :width]
-            inverse = inverse + dot(
-                inverse.astype(bf16), powers[2 * at + half, :, width:].astype(bf16)
-            )
-            top_right = dot3(inverse, angles)
-            flip_right = top_right.T
-            low_right = identity - 0.5 * dot3(angles.T, top_right)
-            top = split(2.0 * inverse - identity)
-            right = split(top_right)
-            flip = split(flip_right)
-            low = split(low_right)
+            top = split(2.0 * inverses[2 * at + half] - identity)
+            right = split(rights[2 * at + half])
+            flip = split(rights[2 * at + half].T)
+            low = split(lows[2 * at + half])
 
             def square(kind, flipped):
                 above, below = (-right[kind], flip[kind]) if flipped else (right[kind], -flip[kind])
@@ -135,6 +166,7 @@
 
             flips[at, half] = left_parts((square(0, True), square(1, True)))
             rotation = right_parts((square(0, False), square(1, False)))
+            turn[slot, half] = rotation
             for members in (pairs[0],) if half == 0 else pairs:
                 rows = jnp.concatenate(
                     [
@@ -153,15 +185,6 @@
                         wide = slice(across * width, (across + 1) * width)
                         mid_high[slot, span(member), span(column)] = middle[0][tall, wide]
                         mid_low[slot, span(member), span(column)] = middle[1][tall, wide]
-            columns = tuple(
-                jnp.concatenate([ref[slot, :, span(first)], ref[slot, :, span(second)]], axis=1)
-                for ref in (vec_high, vec_low)
-            )
-            turned = split(dot(left_parts(columns), rotation))
-            for place, member in enumerate((first, second)):
-                inner = slice(place * width, (place + 1) * width)
-                vec_high[slot, :, span(member)] = turned[0][:, inner]
-                vec_low[slot, :, span(member)] = turned[1][:, inner]
         for at, slot, half in chains:
             order = pairs[0] + pairs[1] if half == 0 else pairs[1]
             rows = tuple(
@@ -222,8 +245,11 @@
         ]
 
         def run(slots):
-            for pairing in pairings:
-                one_round(slots, pairing)
+            for before, pairing in zip((None,) + pairings, pairings):
+                one_round(slots, pairing, before)
+            for slot in slots:
+                for half in range(2):
+                    turn_half(slot, half, pairings[-1])
             for slot in slots:
                 measure(sweep, slot)
 
@@ -260,21 +286,26 @@
             scales = lax.rsqrt(jnp.sqrt(jnp.sqrt(diagonal)))
             vectors = vec_high[slot].astype(f32) + vec_low[slot].astype(f32)
             high, low = split(vectors * scales)
-            left = jnp.concatenate([high, high, low], axis=1)
-            right = jnp.concatenate([high, low, high], axis=1)
-            start = 0
-            for row in range(4):
+            mid_high[slot] = high
+            mid_low[slot] = low
+            for tile in range(2):
+                tall, wide = 2 * width * (tile + 1), pl.ds(2 * width * tile, 2 * width)
+                left = jnp.concatenate(
+                    [mid_high[slot, :tall], mid_high[slot, :tall], mid_low[slot, :tall]], axis=1
+                )
+                right = jnp.concatenate(
+                    [mid_high[slot, wide], mid_low[slot, wide], mid_high[slot, wide]], axis=1
+                )
                 strip = lax.dot_general(
-                    left[row * width : (row + 1) * width],
-                    right[row * width :],
-                    (((1,), (1,)), ((), ())),
-                    preferred_element_type=f32,
+                    left, right, (((1,), (1,)), ((), ())), preferred_element_type=f32
                 ).astype(bf16)
-                for column in range(4 - row):
-                    packed_ref[slot, start : start + width] = strip[
-                        :, column * width : (column + 1) * width
-                    ]
-                    start += width
+                for column in (2 * tile, 2 * tile + 1):
+                    for row in range(column + 1):
+                        start = (4 * row - row * (row - 1) // 2 + column - row) * width
+                        packed_ref[slot, start : start + width] = strip[
+                            row * width : (row + 1) * width,
+                            (column - 2 * tile) * width : (column - 2 * tile + 1) * width,
+                        ]
 
 
 def jacobi(statistics, live_counts, sweeps, packed_rows):
@@ -299,6 +330,7 @@
             pltpu.VMEM((slot_count, size, size), bf16),
             pltpu.VMEM((4, width, width), f32),
             pltpu.VMEM((4, width, 2 * width), f32),
+            pltpu.VMEM((slot_count, 2, 6 * width, 2 * width), bf16),
         ],
         compiler_params=pltpu.CompilerParams(vmem_limit_bytes=24 * 1024 * 1024),
         cost_estimate=pl.CostEstimate(
@@ -555,7 +587,12 @@
     )(packed, peaks, live_counts, slot_row)
 
 
-def update_kernel(whole_ref, grads_ref, updates_ref):
+def update_kernel(whole_ref, grads_ref, peaks_ref, updates_ref, off_ref):
+    @pl.when(pl.program_id(0) == 0)
+    def _():
+        for sweep in range(MAXS):
+            off_ref[sweep] = jnp.max(peaks_ref[sweep : sweep + 1])
+
     width = whole_ref.shape[2]
     for row in range(whole_ref.shape[0]):
         blocks = {}
@@ -577,24 +614,31 @@
         updates_ref[0, row] = dot(grads_ref[0, row], factor).astype(bf16)
 
 
-def update(whole, gradients):
+def update(whole, gradients, peaks):
     row_count, columns, size = gradients.shape[1:]
-    rows = 2
+    rows = 4
     block = pl.BlockSpec((1, rows, columns, size), lambda row: (0, row, 0, 0))
     return pl.pallas_call(
         update_kernel,
         name="update",
         grid=(row_count // rows,),
-        out_shape=jax.ShapeDtypeStruct(gradients.shape, bf16),
-        in_specs=[pl.BlockSpec((rows,) + whole.shape[1:], lambda row: (row, 0, 0)), block],
-        out_specs=block,
+        out_shape=(
+            jax.ShapeDtypeStruct(gradients.shape, bf16),
+            jax.ShapeDtypeStruct((MAXS,), f32),
+        ),
+        in_specs=[
+            pl.BlockSpec((rows,) + whole.shape[1:], lambda row: (row, 0, 0)),
+            block,
+            pl.BlockSpec(memory_space=pltpu.VMEM),
+        ],
+        out_specs=(block, pl.BlockSpec(memory_space=pltpu.SMEM)),
         compiler_params=pltpu.CompilerParams(vmem_limit_bytes=24 * 1024 * 1024),
         cost_estimate=pl.CostEstimate(
             flops=2 * row_count * size * size * columns,
             bytes_accessed=2 * row_count * size * columns,
             transcendentals=0,
         ),
-    )(whole, gradients)
+    )(whole, gradients, peaks)
 
 
 def per_device(peers, groups, statistics, gradients, live_counts, slot_row, sweeps):
@@ -603,8 +647,8 @@
     side = next(edge for edge in range(1, peers) if 2 * edge * edge == peers)
     packed, peaks = jacobi(statistics, live_counts, sweeps, 10 * width)
     whole, top = exchange(packed, peaks, live_counts, slot_row, row_count, side, groups)
-    updates = update(whole, jnp.swapaxes(gradients, 2, 3))
-    return (jnp.swapaxes(updates, 2, 3), top[:, 0])
+    updates, off = update(whole, jnp.swapaxes(gradients, 2, 3), top)
+    return (jnp.swapaxes(updates, 2, 3), off)
 
 
 def solution(mesh):

time: 96.7 us -> 86.7 us (0.90)
  Pallas kernels: 92.8 us -> 82.9 us
    pallas_call x1, Pallas kernels: 44.7 us -> 13.5 us  [jacobi(): pl.pallas_call(jacobi_kernel, name='jacobi', out_shape=(jax.ShapeDtypeStr...]
    pallas_call x1, Pallas kernels: 41 us -> 63.2 us  [exchange(): pl.pallas_call(functools.partial(exchange_kernel, side, groups), name='ex...]
    pallas_call x1, Pallas kernels: 7.05 us -> 6.08 us  [update(): pl.pallas_call(update_kernel, name='update', grid=(row_count // rows,), o...]
    unnamed x14 -> x12, local copies, waits for them, and re-layouts: 2.91 us -> 2.91 us
where the time goes in v3:
time: 86.7 us; the launch traced here: 86.5 us
  Pallas kernels  82.9 us (96%)
  local copies, waits for them, and re-layouts  2.91 us (3%)
    pallas_call x1, Pallas kernels, exchange(): pl.pallas_call(functools.partial(exchange_kernel, side, groups), name='ex...  63.2 us
    pallas_call x1, Pallas kernels, jacobi(): pl.pallas_call(jacobi_kernel, name='jacobi', out_shape=(jax.ShapeDtypeStr...  13.5 us
    pallas_call x1, Pallas kernels, update(): pl.pallas_call(update_kernel, name='update', grid=(row_count // rows,), o...  6.08 us
    unnamed x12, local copies, waits for them, and re-layouts  2.91 us

profile of v3, /device:TPU:1, one launch (start us, length us, event | category | flops | bytes accessed | tf_op | source)
XLA Modules:
  0.0 86.5 jit_solution(7160287558319513941)
XLA Ops:
  0.6 0.0 copy-start
  0.6 1.6 %copy-done = f32[1,2,512,512]{3,2,1,0:T(8,128)S(1)} copy-done((f32[1,2,512,512]{3,2,1,0:T(8,128)S(1)}, f32[1,2,512,512]{3,2,1,0:T(8,128)}, u32[]{:S(2)}) %copy-start) | copy-done | bytes 2097176
  2.2 0.0 copy-start.1
  2.2 0.7 copy-done.1
  2.9 0.0 copy-start.2
  2.9 0.7 copy-done.2
  3.5 0.0 copy-start.3
  3.5 0.0 slice-start
  3.5 13.5 %jacobi.1 = (bf16[2,1280,128]{2,1,0:T(8,128)(2,1)S(1)}, f32[2,128]{1,0:T(2,128)S(1)}) custom-call(f32[1,2,512,512]{3,2,1,0:T(8,128)S(1)} %copy-done, s32[1,32]{1,0:T(1,128)S(1)} %copy-done.2, s32[1,2]{1,0:T(1,128)S(1)} %copy-done.1), custom_call_target="tpu_custom_call" | custom-call | flops 10000000000 | bytes 2097152 | tf_op jit(solution)/shard_map/jacobi/pallas_call | solution.py:316
  17.1 0.0 slice-start.1
  17.1 0.0 copy-done.3
  17.1 63.2 %exchange.1 = (bf16[16,1280,128]{2,1,0:T(8,128)(2,1)S(1)}, f32[2,128]{1,0:T(2,128)S(1)}) custom-call(bf16[2,1280,128]{2,1,0:T(8,128)(2,1)S(1)} %get-tuple-element.8.packed_ref, f32[2,128]{1,0:T(2,128)S(1)} %get-tuple-element.9.peaks_ref, s32[1,32]{1,0:T(1,128)S(1)} %copy-done.2, s32[1,64]{1,0:T(1,128)S(1)} %copy-done.3), custom_call_target="tpu_custom_call" | custom-call | flops 10000000000 | bytes 5242880 | tf_op jit(solution)/shard_map/exchange/pallas_call | solution.py:563
  80.4 0.0 slice-done
  80.4 0.0 slice-done.1
  80.4 6.1 %update.1 = (bf16[1,16,448,512]{3,2,1,0:T(8,128)(2,1)}, f32[2]{0:T(128)}) custom-call(bf16[16,1280,128]{2,1,0:T(8,128)(2,1)S(1)} %get-tuple-element.10.whole_ref, bf16[1,16,448,512]{3,2,1,0:T(8,128)(2,1)S(1)} %bitcast.4, f32[2,128]{1,0:T(2,128)S(1)} %get-tuple-element.11.peaks_ref), custom_call_target="tpu_custom_call" | custom-call | flops 3758096384 | bytes 7340032 | tf_op jit(solution)/shard_map/update/pallas_call | solution.py:621
  (1 shorter events, 0.0 us)
Async XLA Ops:
  0.6 1.6 %copy-start = (f32[1,2,512,512]{3,2,1,0:T(8,128)S(1)}, f32[1,2,512,512]{3,2,1,0:T(8,128)}, u32[]{:S(2)}) copy-start(f32[1,2,512,512]{3,2,1,0:T(8,128)} %stats_ref.1) | copy-start | bytes 6291460
  2.2 0.7 copy-start.1
  2.9 0.7 copy-start.2
  3.5 13.6 %copy-start.3 = (s32[1,64]{1,0:T(1,128)S(1)}, s32[1,64]{1,0:T(1,128)}, u32[]{:S(2)}) copy-start(s32[1,64]{1,0:T(1,128)} %rows_ref.1) | copy-start | bytes 772
  3.5 76.8 %slice-start = ((s8[7340032]{0:T(1024)(128)(4,1)}), s8[4194304]{0:T(1024)(128)(4,1)S(1)}, s32[]{:S(2)}) async-start(s8[7340032]{0:T(1024)(128)(4,1)} %bitcast.2), calls=%async_computation | async-start | bytes 8388608
  17.1 63.3 %slice-start.1 = ((s8[7340032]{0:T(1024)(128)(4,1)}), s8[3145728]{0:T(1024)(128)(4,1)S(1)}, s32[]{:S(2)}) async-start(s8[7340032]{0:T(1024)(128)(4,1)} %bitcast.2), calls=%async_computation.1 | async-start | bytes 6291456

commit v4 on v3

--- a/solution.py
+++ b/solution.py
@@ -10,6 +10,7 @@
 MAXS = 2
 
 damping = 0.01
+apart = ((0, 1), (0, 2), (0, 3), (1, 2), (1, 3), (2, 3))
 pairings = ((0, 1, 2, 3), (0, 2, 1, 3), (0, 3, 1, 2))
 kappa_steps = (1.16, 1.74, 3.17, 6.2, 12.3, 24.5, 49.0, 98.0, 196.0)
 bf16 = jnp.bfloat16
@@ -42,6 +43,11 @@
 def eye_mask(size):
     shape = (size, size)
     return lax.broadcasted_iota(jnp.int32, shape, 0) == lax.broadcasted_iota(jnp.int32, shape, 1)
+
+
+def upper_mask(size):
+    shape = (size, size)
+    return lax.broadcasted_iota(jnp.int32, shape, 0) <= lax.broadcasted_iota(jnp.int32, shape, 1)
 
 
 def angles_of(lower, coupling, upper, on_diagonal):
@@ -62,6 +68,7 @@
     rank = lax.axis_index("blk")
     own_live = counts_ref[0, rank]
     on_diagonal = eye_mask(width)
+    upper = upper_mask(width)
     identity = jnp.where(on_diagonal, 1.0, 0.0).astype(f32)
 
     def span(member):
@@ -225,9 +232,9 @@
         total = off_total + jnp.sum(inside, axis=1, keepdims=True)
         norm = jnp.broadcast_to(jnp.sqrt(off_total / total), (1, width))
         row = pl.ds(sweep, 1)
-        off_ref[row, :] = jnp.maximum(off_ref[row, :], norm)
-
-    off_ref[...] = jnp.zeros_like(off_ref)
+        off_ref[0, row, :] = jnp.maximum(off_ref[0, row, :], norm)
+
+    off_ref[0] = jnp.zeros(off_ref.shape[1:], f32)
     ident_rows = jnp.where(eye_mask(size), 1.0, 0.0).astype(bf16)
 
     for slot in range(slot_count):
@@ -298,14 +305,28 @@
                 )
                 strip = lax.dot_general(
                     left, right, (((1,), (1,)), ((), ())), preferred_element_type=f32
+                )
+
+                def block(row, column):
+                    across = column - 2 * tile
+                    return strip[
+                        row * width : (row + 1) * width, across * width : (across + 1) * width
+                    ]
+
+                first, second = block(2 * tile, 2 * tile), block(2 * tile + 1, 2 * tile + 1)
+                packed_ref[slot, tile * width : (tile + 1) * width] = jnp.where(
+                    upper, first, second
                 ).astype(bf16)
-                for column in (2 * tile, 2 * tile + 1):
-                    for row in range(column + 1):
-                        start = (4 * row - row * (row - 1) // 2 + column - row) * width
-                        packed_ref[slot, start : start + width] = strip[
-                            row * width : (row + 1) * width,
-                            (column - 2 * tile) * width : (column - 2 * tile + 1) * width,
-                        ]
+                off_ref[1 + slot, tile : tile + 1] = jnp.sum(
+                    jnp.where(on_diagonal, second.astype(bf16).astype(f32), 0.0),
+                    axis=0,
+                    keepdims=True,
+                )
+                for start, (row, column) in enumerate(apart, 2):
+                    if column // 2 == tile:
+                        packed_ref[slot, start * width : (start + 1) * width] = block(
+                            row, column
+                        ).astype(bf16)
 
 
 def jacobi(statistics, live_counts, sweeps, packed_rows):
@@ -318,7 +339,7 @@
         name="jacobi",
         out_shape=(
             jax.ShapeDtypeStruct((slot_count, packed_rows, width), bf16),
-            jax.ShapeDtypeStruct((MAXS, width), f32),
+            jax.ShapeDtypeStruct((1 + slot_count, 2, width), f32),
         ),
         in_specs=[vmem, smem, smem],
         out_specs=(vmem, vmem),
@@ -340,7 +361,7 @@
 
 
 def exchange_kernel(
-    side, groups, packed_ref, peaks_ref, counts_ref, rows_ref, whole_ref, off_ref,
+    side, groups, packed_ref, peaks_ref, counts_ref, rows_ref, whole_ref, edges_ref, off_ref,
     arrived, mine, peak_in, peak_own, peak_out,
     send_one, recv_one, send_two, recv_two, send_near, recv_near, send_peak, recv_peak, send_top, recv_top,
 ):
@@ -392,11 +413,12 @@
         )
         peaks.append(
             remote(
-                peaks_ref, peak_in.at[step], send_peak.at[step], recv_peak.at[step], "blk", target
+                peaks_ref, peak_in.at[rank], send_peak.at[step], recv_peak.at[step], "blk", target
             )
         )
     for copy in firsts + peaks:
         copy.start()
+    peak_in[rank] = peaks_ref[...]
     for local in range(slot_count):
         arrived[rank * slot_count + local] = packed_ref[local, strip(rank)]
 
@@ -505,10 +527,13 @@
     for route in routes:
         spread(route, 0)
     whole_ref[:, strip(rank)] = mine[...]
-    top = peaks_ref[...]
-    for step, copy in enumerate(peaks, 1):
+    for copy in peaks:
         copy.wait_recv()
-        top = jnp.maximum(top, peak_in[step])
+    top = peak_in[0, 0]
+    for owner in range(1, peers):
+        top = jnp.maximum(top, peak_in[owner, 0])
+    for row in range(row_count):
+        edges_ref[row] = peak_in[places[row] // slot_count, 1 + lax.rem(places[row], slot_count)]
     peak_own[...] = top
     tops = []
     for step in range(1, groups):
@@ -565,16 +590,17 @@
         name="exchange",
         out_shape=(
             jax.ShapeDtypeStruct((row_count, packed_rows, width), bf16),
-            jax.ShapeDtypeStruct(peaks.shape, f32),
+            jax.ShapeDtypeStruct((row_count,) + peaks.shape[1:], f32),
+            jax.ShapeDtypeStruct(peaks.shape[1:], f32),
         ),
         in_specs=[vmem, vmem, smem, smem],
-        out_specs=(vmem, vmem),
+        out_specs=(vmem, vmem, vmem),
         scratch_shapes=[
             pltpu.VMEM((peers * slot_count, share, width), bf16),
             pltpu.VMEM((row_count, share, width), bf16),
             pltpu.VMEM((peers,) + peaks.shape, f32),
-            pltpu.VMEM(peaks.shape, f32),
-            pltpu.VMEM((groups,) + peaks.shape, f32),
+            pltpu.VMEM(peaks.shape[1:], f32),
+            pltpu.VMEM((groups,) + peaks.shape[1:], f32),
             dma((peers,)), dma((peers,)), dma((40,)), dma((40,)), dma((32,)),
             dma((32,)), dma((peers,)), dma((peers,)), dma((groups,)), dma((groups,)),
         ],
@@ -587,34 +613,49 @@
     )(packed, peaks, live_counts, slot_row)
 
 
-def update_kernel(whole_ref, grads_ref, peaks_ref, updates_ref, off_ref):
+def update_kernel(whole_ref, edges_ref, grads_ref, peaks_ref, updates_ref, off_ref):
     @pl.when(pl.program_id(0) == 0)
     def _():
         for sweep in range(MAXS):
             off_ref[sweep] = jnp.max(peaks_ref[sweep : sweep + 1])
 
     width = whole_ref.shape[2]
+    upper, on_diagonal = upper_mask(width), eye_mask(width)
     for row in range(whole_ref.shape[0]):
         blocks = {}
-        start = 0
-        for above in range(4):
-            for below in range(above, 4):
-                block = whole_ref[row, start : start + width]
-                start += width
-                blocks[above, below] = block
-                if above != below:
-                    blocks[below, above] = block.T
-        factor = jnp.concatenate(
-            [
-                jnp.concatenate([blocks[above, below] for below in range(4)], axis=1)
-                for above in range(4)
-            ],
-            axis=0,
-        )
-        updates_ref[0, row] = dot(grads_ref[0, row], factor).astype(bf16)
-
-
-def update(whole, gradients, peaks):
+        for start, where in enumerate(apart, 2):
+            blocks[where] = whole_ref[row, start * width : (start + 1) * width]
+        for side, above in enumerate((0, 2)):
+            both = whole_ref[row, side * width : (side + 1) * width]
+            flipped = both.T
+            edge = jnp.where(on_diagonal, edges_ref[row, side : side + 1], 0.0).astype(bf16)
+            blocks[above, above] = jnp.where(upper, both, flipped)
+            blocks[above + 1, above + 1] = jnp.where(
+                on_diagonal, edge, jnp.where(upper, flipped, both)
+            )
+            blocks[above + 1, above] = blocks[above, above + 1].T
+
+        def tile(first, second):
+            return jnp.concatenate(
+                [
+                    jnp.concatenate([blocks[above, below] for below in (second, second + 1)], axis=1)
+                    for above in (first, first + 1)
+                ],
+                axis=0,
+            )
+
+        corner = tile(0, 2)
+        left, right = grads_ref[0, row, :, : 2 * width], grads_ref[0, row, :, 2 * width :]
+        turned = lax.dot_general(
+            right, corner, (((1,), (1,)), ((), ())), preferred_element_type=f32
+        )
+        updates_ref[0, row, :, : 2 * width] = (dot(left, tile(0, 0)) + turned).astype(bf16)
+        updates_ref[0, row, :, 2 * width :] = (dot(left, corner) + dot(right, tile(2, 2))).astype(
+            bf16
+        )
+
+
+def update(whole, edges, gradients, peaks):
     row_count, columns, size = gradients.shape[1:]
     rows = 4
     block = pl.BlockSpec((1, rows, columns, size), lambda row: (0, row, 0, 0))
@@ -628,6 +669,7 @@
         ),
         in_specs=[
             pl.BlockSpec((rows,) + whole.shape[1:], lambda row: (row, 0, 0)),
+            pl.BlockSpec((rows,) + edges.shape[1:], lambda row: (row, 0, 0)),
             block,
             pl.BlockSpec(memory_space=pltpu.VMEM),
         ],
@@ -638,16 +680,16 @@
             bytes_accessed=2 * row_count * size * columns,
             transcendentals=0,
         ),
-    )(whole, gradients, peaks)
+    )(whole, edges, gradients, peaks)
 
 
 def per_device(peers, groups, statistics, gradients, live_counts, slot_row, sweeps):
     row_count, size = gradients.shape[1], gradients.shape[2]
     width = size // 4
     side = next(edge for edge in range(1, peers) if 2 * edge * edge == peers)
-    packed, peaks = jacobi(statistics, live_counts, sweeps, 10 * width)
-    whole, top = exchange(packed, peaks, live_counts, slot_row, row_count, side, groups)
-    updates, off = update(whole, jnp.swapaxes(gradients, 2, 3), top)
+    packed, peaks = jacobi(statistics, live_counts, sweeps, 8 * width)
+    whole, edges, top = exchange(packed, peaks, live_counts, slot_row, row_count, side, groups)
+    updates, off = update(whole, edges, jnp.swapaxes(gradients, 2, 3), top)
     return (jnp.swapaxes(updates, 2, 3), off)
 
 

time: 86.7 us -> 83.7 us (0.965)
  the two profiles are of different devices: /device:TPU:1 before, /device:TPU:25 now
where the time goes in v4:
time: 83.7 us
  Pallas kernels  80.1 us (96%)
  local copies, waits for them, and re-layouts  2.91 us (3%)
    pallas_call x1, Pallas kernels, exchange(): pl.pallas_call(functools.partial(exchange_kernel, side, groups), name='ex...  59.7 us
    pallas_call x1, Pallas kernels, jacobi(): pl.pallas_call(jacobi_kernel, name='jacobi', out_shape=(jax.ShapeDtypeStr...  14 us
    pallas_call x1, Pallas kernels, update(): pl.pallas_call(update_kernel, name='update', grid=(row_count // rows,), o...  6.33 us
    unnamed x12, local copies, waits for them, and re-layouts  2.91 us

profile of v4, /device:TPU:25, one launch (start us, length us, event | category | flops | bytes accessed | tf_op | source)
XLA Modules:
  0.0 83.7 jit_solution(4370444514927996531)
XLA Ops:
  0.6 0.0 copy-start
  0.6 1.6 %copy-done = f32[1,2,512,512]{3,2,1,0:T(8,128)S(1)} copy-done((f32[1,2,512,512]{3,2,1,0:T(8,128)S(1)}, f32[1,2,512,512]{3,2,1,0:T(8,128)}, u32[]{:S(2)}) %copy-start) | copy-done | bytes 2097176
  2.2 0.0 copy-start.1
  2.2 0.7 copy-done.1
  2.9 0.0 copy-start.2
  2.9 0.7 copy-done.2
  3.5 0.0 copy-start.3
  3.5 0.0 slice-start
  3.5 14.0 %jacobi.1 = (bf16[2,1024,128]{2,1,0:T(8,128)(2,1)S(1)}, f32[3,2,128]{2,1,0:T(2,128)S(1)}) custom-call(f32[1,2,512,512]{3,2,1,0:T(8,128)S(1)} %copy-done, s32[1,32]{1,0:T(1,128)S(1)} %copy-done.2, s32[1,2]{1,0:T(1,128)S(1)} %copy-done.1), custom_call_target="tpu_custom_call" | custom-call | flops 10000000000 | bytes 2097152 | tf_op jit(solution)/shard_map/jacobi/pallas_call | solution.py:337
  17.6 0.0 copy-done.3
  17.6 0.0 slice-start.1
  17.6 59.7 %exchange.1 = (bf16[16,1024,128]{2,1,0:T(8,128)(2,1)S(1)}, f32[16,2,128]{2,1,0:T(2,128)S(1)}, f32[2,128]{1,0:T(2,128)S(1)}) custom-call(bf16[2,1024,128]{2,1,0:T(8,128)(2,1)S(1)} %get-tuple-element.9.packed_ref, f32[3,2,128]{2,1,0:T(2,128)S(1)} %get-tuple-element.10.peaks_ref, s32[1,32]{1,0:T(1,128)S(1)} %copy-done.2, s32[1,64]{1,0:T(1,128)S(1)} %copy-done.3), custom_call_target="tpu_custom_call" | custom-call | flops 10000000000 | bytes 4194304 | tf_op jit(solution)/shard_map/exchange/pallas_call | solution.py:588
  77.3 0.0 slice-done
  77.3 0.0 slice-done.1
  77.3 6.3 %update.1 = (bf16[1,16,448,512]{3,2,1,0:T(8,128)(2,1)}, f32[2]{0:T(128)}) custom-call(bf16[16,1024,128]{2,1,0:T(8,128)(2,1)S(1)} %get-tuple-element.11.whole_ref, f32[16,2,128]{2,1,0:T(2,128)S(1)} %get-tuple-element.12.edges_ref, bf16[1,16,448,512]{3,2,1,0:T(8,128)(2,1)S(1)} %bitcast.4, f32[2,128]{1,0:T(2,128)S(1)} %get-tuple-element.13.peaks_ref), custom_call_target="tpu_custom_call" | custom-call | flops 3758096384 | bytes 7340032 | tf_op jit(solution)/shard_map/update/pallas_call | solution.py:662
  (1 shorter events, 0.0 us)
Async XLA Ops:
  0.6 1.6 %copy-start = (f32[1,2,512,512]{3,2,1,0:T(8,128)S(1)}, f32[1,2,512,512]{3,2,1,0:T(8,128)}, u32[]{:S(2)}) copy-start(f32[1,2,512,512]{3,2,1,0:T(8,128)} %stats_ref.1) | copy-start | bytes 6291460
  2.2 0.7 copy-start.1
  2.9 0.7 copy-start.2
  3.5 14.0 %copy-start.3 = (s32[1,64]{1,0:T(1,128)S(1)}, s32[1,64]{1,0:T(1,128)}, u32[]{:S(2)}) copy-start(s32[1,64]{1,0:T(1,128)} %rows_ref.1) | copy-start | bytes 772
  3.5 73.8 %slice-start = ((s8[7340032]{0:T(1024)(128)(4,1)}), s8[4194304]{0:T(1024)(128)(4,1)S(1)}, s32[]{:S(2)}) async-start(s8[7340032]{0:T(1024)(128)(4,1)} %bitcast.2), calls=%async_computation | async-start | bytes 8388608
  17.6 59.7 %slice-start.1 = ((s8[7340032]{0:T(1024)(128)(4,1)}), s8[3145728]{0:T(1024)(128)(4,1)S(1)}, s32[]{:S(2)}) async-start(s8[7340032]{0:T(1024)(128)(4,1)} %bitcast.2), calls=%async_computation.1 | async-start | bytes 6291456

commit v5 on v4

--- a/solution.py
+++ b/solution.py
@@ -386,9 +386,22 @@
         )
 
     barrier = pltpu.get_barrier_semaphore()
-    for step in range(1, peers):
+    ring = [(lead, lag) for lead in range(side) for lag in range(side)]
+    offsets = [(lead, lag, flip) for lead, lag in ring for flip in range(2)]
+
+    def hops(offset):
+        lead, lag, flip = offset
+        return -(min(lead, side - lead) + min(lag, side - lag)), -flip
+
+    targets = [
+        (
+            lax.rem(place_x + lead, side) * side + lax.rem(place_z + lag, side)
+        ) * 2 + (1 - core if flip else core)
+        for lead, lag, flip in sorted(offsets, key=hops)[:-1]
+    ]
+    for target in targets:
         pl.semaphore_signal(
-            barrier, inc=1, device_id={"blk": lax.rem(rank + step, peers)},
+            barrier, inc=1, device_id={"blk": target},
             device_id_type=pl.DeviceIdType.MESH,
         )
     for step in range(1, groups):
@@ -403,8 +416,7 @@
 
     firsts, peaks = [], []
     own_slots = pl.ds(rank * slot_count, slot_count)
-    for step in range(1, peers):
-        target = lax.rem(rank + step, peers)
+    for step, target in enumerate(targets):
         firsts.append(
             remote(
                 packed_ref.at[:, strip(target)],
@@ -613,15 +625,19 @@
     )(packed, peaks, live_counts, slot_row)
 
 
-def update_kernel(whole_ref, edges_ref, grads_ref, peaks_ref, updates_ref, off_ref):
-    @pl.when(pl.program_id(0) == 0)
-    def _():
-        for sweep in range(MAXS):
-            off_ref[sweep] = jnp.max(peaks_ref[sweep : sweep + 1])
-
+def update_kernel(
+    whole_ref, edges_ref, grads_ref, peaks_ref, updates_ref, off_ref, done, sent
+):
     width = whole_ref.shape[2]
+    row_count = whole_ref.shape[0]
     upper, on_diagonal = upper_mask(width), eye_mask(width)
-    for row in range(whole_ref.shape[0]):
+    for sweep in range(MAXS):
+        off_ref[sweep] = jnp.max(peaks_ref[sweep : sweep + 1])
+
+    def leave(row):
+        return pltpu.make_async_copy(done.at[row], updates_ref.at[0, row], sent.at[row])
+
+    def one_row(row):
         blocks = {}
         for start, where in enumerate(apart, 2):
             blocks[where] = whole_ref[row, start * width : (start + 1) * width]
@@ -649,31 +665,36 @@
         turned = lax.dot_general(
             right, corner, (((1,), (1,)), ((), ())), preferred_element_type=f32
         )
-        updates_ref[0, row, :, : 2 * width] = (dot(left, tile(0, 0)) + turned).astype(bf16)
-        updates_ref[0, row, :, 2 * width :] = (dot(left, corner) + dot(right, tile(2, 2))).astype(
+        done[row, :, : 2 * width] = (dot(left, tile(0, 0)) + turned).astype(bf16)
+        done[row, :, 2 * width :] = (dot(left, corner) + dot(right, tile(2, 2))).astype(
             bf16
         )
+
+    for row in range(row_count):
+        one_row(row)
+        if row:
+            leave(row - 1).start()
+    leave(row_count - 1).start()
+    for row in range(row_count):
+        leave(row).wait()
 
 
 def update(whole, edges, gradients, peaks):
     row_count, columns, size = gradients.shape[1:]
-    rows = 4
-    block = pl.BlockSpec((1, rows, columns, size), lambda row: (0, row, 0, 0))
+    vmem = pl.BlockSpec(memory_space=pltpu.VMEM)
     return pl.pallas_call(
         update_kernel,
         name="update",
-        grid=(row_count // rows,),
         out_shape=(
             jax.ShapeDtypeStruct(gradients.shape, bf16),
             jax.ShapeDtypeStruct((MAXS,), f32),
         ),
-        in_specs=[
-            pl.BlockSpec((rows,) + whole.shape[1:], lambda row: (row, 0, 0)),
-            pl.BlockSpec((rows,) + edges.shape[1:], lambda row: (row, 0, 0)),
-            block,
-            pl.BlockSpec(memory_space=pltpu.VMEM),
+        in_specs=[vmem] * 4,
+        out_specs=(pl.BlockSpec(memory_space=pl.ANY), pl.BlockSpec(memory_space=pltpu.SMEM)),
+        scratch_shapes=[
+            pltpu.VMEM(gradients.shape[1:], bf16),
+            pltpu.SemaphoreType.DMA((row_count,)),
         ],
-        out_specs=(block, pl.BlockSpec(memory_space=pltpu.SMEM)),
         compiler_params=pltpu.CompilerParams(vmem_limit_bytes=24 * 1024 * 1024),
         cost_estimate=pl.CostEstimate(
             flops=2 * row_count * size * size * columns,

time: 83.7 us -> 80.7 us (0.964)
  the two profiles are of different devices: /device:TPU:25 before, /device:TPU:1 now
where the time goes in v5:
time: 80.7 us; the launch traced here: 79.5 us
  Pallas kernels  75.8 us (94%)
  local copies, waits for them, and re-layouts  2.91 us (4%)
  between operations  0.86 us (1%)
    pallas_call x1, Pallas kernels, exchange(): pl.pallas_call(functools.partial(exchange_kernel, side, groups), name='ex...  69.2 us
    pallas_call x1, Pallas kernels, update(): pl.pallas_call(update_kernel, name='update', out_shape=(jax.ShapeDtypeStr...  5.71 us
    unnamed x12, local copies, waits for them, and re-layouts  2.91 us

profile of v5, /device:TPU:1, one launch (start us, length us, event | category | flops | bytes accessed | tf_op | source)
XLA Modules:
  0.0 79.5 jit_solution(7436688165501344305)
XLA Ops:
  0.6 0.0 copy-start
  0.6 1.6 %copy-done = f32[1,2,512,512]{3,2,1,0:T(8,128)S(1)} copy-done((f32[1,2,512,512]{3,2,1,0:T(8,128)S(1)}, f32[1,2,512,512]{3,2,1,0:T(8,128)}, u32[]{:S(2)}) %copy-start) | copy-done | bytes 2097176
  2.2 0.0 copy-start.1
  2.2 0.7 copy-done.1
  2.9 0.0 copy-start.2
  2.9 0.7 copy-done.2
  3.5 0.0 copy-start.3
  3.5 0.0 slice-start
  3.5 0.8 %jacobi.1 = (bf16[2,1024,128]{2,1,0:T(8,128)(2,1)S(1)}, f32[3,2,128]{2,1,0:T(2,128)S(1)}) custom-call(f32[1,2,512,512]{3,2,1,0:T(8,128)S(1)} %copy-done, s32[1,32]{1,0:T(1,128)S(1)} %copy-done.2, s32[1,2]{1,0:T(1,128)S(1)} %copy-done.1), custom_call_target="tpu_custom_call" | custom-call | flops 10000000000 | bytes 2097152 | tf_op jit(solution)/shard_map/jacobi/pallas_call | solution.py:337
  4.4 0.0 copy-done.3
  4.4 0.0 slice-start.1
  4.4 69.2 %exchange.1 = (bf16[16,1024,128]{2,1,0:T(8,128)(2,1)S(1)}, f32[16,2,128]{2,1,0:T(2,128)S(1)}, f32[2,128]{1,0:T(2,128)S(1)}) custom-call(bf16[2,1024,128]{2,1,0:T(8,128)(2,1)S(1)} %get-tuple-element.9.packed_ref, f32[3,2,128]{2,1,0:T(2,128)S(1)} %get-tuple-element.10.peaks_ref, s32[1,32]{1,0:T(1,128)S(1)} %copy-done.2, s32[1,64]{1,0:T(1,128)S(1)} %copy-done.3), custom_call_target="tpu_custom_call" | custom-call | flops 10000000000 | bytes 4194304 | tf_op jit(solution)/shard_map/exchange/pallas_call | solution.py:600
  73.6 0.0 slice-done
  73.7 0.0 slice-done.1
  73.7 5.7 %update.1 = (bf16[1,16,448,512]{3,2,1,0:T(8,128)(2,1)}, f32[2]{0:T(128)}) custom-call(bf16[16,1024,128]{2,1,0:T(8,128)(2,1)S(1)} %get-tuple-element.11.whole_ref, f32[16,2,128]{2,1,0:T(2,128)S(1)} %get-tuple-element.12.edges_ref, bf16[1,16,448,512]{3,2,1,0:T(8,128)(2,1)S(1)} %bitcast.4, f32[2,128]{1,0:T(2,128)S(1)} %get-tuple-element.13.peaks_ref), custom_call_target="tpu_custom_call" | custom-call | flops 3758096384 | bytes 7340032 | tf_op jit(solution)/shard_map/update/pallas_call | solution.py:685
  (1 shorter events, 0.0 us)
Async XLA Ops:
  0.6 1.6 %copy-start = (f32[1,2,512,512]{3,2,1,0:T(8,128)S(1)}, f32[1,2,512,512]{3,2,1,0:T(8,128)}, u32[]{:S(2)}) copy-start(f32[1,2,512,512]{3,2,1,0:T(8,128)} %stats_ref.1) | copy-start | bytes 6291460
  2.2 0.7 copy-start.1
  2.9 0.7 copy-start.2
  3.5 0.8 %copy-start.3 = (s32[1,64]{1,0:T(1,128)S(1)}, s32[1,64]{1,0:T(1,128)}, u32[]{:S(2)}) copy-start(s32[1,64]{1,0:T(1,128)} %rows_ref.1) | copy-start | bytes 772
  3.5 70.1 %slice-start = ((s8[7340032]{0:T(1024)(128)(4,1)}), s8[4194304]{0:T(1024)(128)(4,1)S(1)}, s32[]{:S(2)}) async-start(s8[7340032]{0:T(1024)(128)(4,1)} %bitcast.2), calls=%async_computation | async-start | bytes 8388608
  4.4 69.3 %slice-start.1 = ((s8[7340032]{0:T(1024)(128)(4,1)}), s8[3145728]{0:T(1024)(128)(4,1)S(1)}, s32[]{:S(2)}) async-start(s8[7340032]{0:T(1024)(128)(4,1)} %bitcast.2), calls=%async_computation.1 | async-start | bytes 6291456
